TPU v7x, 32 devices: a whole 2x2x4 slice. The times are simulated.
32 devices in a mesh: dp: 8 (over z, y), tensor: 4 (over x, core).
Axes of the slice: x: 2, y: 2, z: 4, core: 2. Of those that a mesh axis runs over, the one named last changes fastest.
Arguments:
- inputs: bfloat16 [8192, 1152], P(('dp', 'tensor')), may hold values from -6 to 6
- segments: int32 [8192], P('dp'), may hold values from 0 to 16, as said below
- w_query: bfloat16 [1152, 1024], P('dp', 'tensor'), may hold values from -0.1875 to 0.1875
- w_key: bfloat16 [1152, 256], P('dp'), may hold values from -0.1875 to 0.1875
- w_value: bfloat16 [1152, 256], P('dp'), may hold values from -0.1875 to 0.1875
- w_out: bfloat16 [1024, 1152], P('tensor', 'dp'), may hold values from -0.375 to 0.375
- g_in: bfloat16 [1152], P('dp'), may hold values from 0.25 to 1.75
- g_attn: bfloat16 [1152], P('dp'), may hold values from 0.25 to 1.75
- g_query: bfloat16 [256], replicated, may hold values from 0.25 to 1.75
- g_key: bfloat16 [256], replicated, may hold values from 0.25 to 1.75
- w_gate: bfloat16 [1152, 6912], P('dp', 'tensor'), may hold values from -0.1875 to 0.1875
- w_up: bfloat16 [1152, 6912], P('dp', 'tensor'), may hold values from -0.1875 to 0.1875
- w_down: bfloat16 [6912, 1152], P('tensor', 'dp'), may hold values from -0.078125 to 0.078125
- g_pre: bfloat16 [1152], P('dp'), may hold values from 0.25 to 1.75
- g_post: bfloat16 [1152], P('dp'), may hold values from 0.25 to 1.75
- cotangent: bfloat16 [8192, 1152], P(('dp', 'tensor')), may hold values from -6 to 6
Outputs:
- output: bfloat16 [8192, 1152], P(('dp', 'tensor'))
- d_inputs: bfloat16 [8192, 1152], P(('dp', 'tensor'))
- grad_query: float32 [1152, 1024], P('dp', 'tensor')
- grad_key: float32 [1152, 256], P(('dp', 'tensor'))
- grad_value: float32 [1152, 256], P(('dp', 'tensor'))
- grad_out: float32 [1024, 1152], P('tensor', 'dp')
- grad_g_in: float32 [1152], P(('dp', 'tensor'))
- grad_g_attn: float32 [1152], P(('dp', 'tensor'))
- grad_g_query: float32 [256], P(('dp', 'tensor'))
- grad_g_key: float32 [256], P(('dp', 'tensor'))
- grad_gate: float32 [1152, 6912], P('dp', 'tensor')
- grad_up: float32 [1152, 6912], P('dp', 'tensor')
- grad_down: float32 [6912, 1152], P('tensor', 'dp')
- grad_g_pre: float32 [1152], P(('dp', 'tensor'))
- grad_g_post: float32 [1152], P(('dp', 'tensor'))
Inputs may be any that keep to these rules, and one draw needn't show every extreme that they name: `segments`: within each block of 1024 rows segment numbers start at 0 and rise by one at the first row of each packed sequence; a sequence starts at every multiple of 512 rows, so none is longer than 512. Every block holds one sequence of exactly 512 rows, and each of its other spans of 512 rows starting at a multiple of 512 holds exactly 16 sequences of uneven lengths.
All inputs are finite; a program needn't handle non-finite values.
Results may differ from a plain program's by a relative error of at most 0.02.
Values may be sent and summed in bfloat16 or wider, within the bound.
A program may use at most 192 MiB of HBM per device.

v0:
```python
from functools import partial

import jax
import jax.numpy as jnp
from jax import lax
from jax.sharding import PartitionSpec as P

HD = 256
SEGMAX = 512


EPSILON = 1e-06
THETA = 1000000.0
NEG_LARGE = -1e30


def rms_scale(values, gain_vec):
    inverse = lax.rsqrt(jnp.mean(values * values, axis=-1, keepdims=True) + EPSILON)
    return values * inverse * gain_vec


def gelu_product(gate_proj, up_proj):
    return jax.nn.gelu(gate_proj, approximate=True) * up_proj


def rows_product(left, right):
    return lax.dot_general(
        left, right, (((0,), (0,)), ((), ())), preferred_element_type=jnp.float32
    )


def cols_product(left, right):
    return lax.dot_general(
        left, right, (((1,), (1,)), ((), ())), preferred_element_type=jnp.float32
    )


def plain_product(left, right):
    return jnp.dot(left, right, preferred_element_type=jnp.float32)


def rotary_tables(segments):
    count = segments.shape[0]
    row_index = jnp.arange(count, dtype=jnp.int32)
    previous = jnp.concatenate([jnp.full((1,), -1, jnp.int32), segments[:-1]])
    starts = jnp.where(segments != previous, row_index, jnp.zeros_like(row_index))
    seq_start = lax.cummax(starts, axis=0)
    position = (row_index - seq_start).astype(jnp.float32)
    half_width = HD // 2
    exponent = -2.0 * jnp.arange(half_width, dtype=jnp.float32) / HD
    inverse = jnp.power(jnp.float32(THETA), exponent)
    angles = position[:, None] * inverse[None, :]
    cosine = jnp.concatenate([jnp.cos(angles), jnp.cos(angles)], axis=1)
    sine_tab = jnp.concatenate([jnp.sin(angles), jnp.sin(angles)], axis=1)
    return (cosine, sine_tab)


def prepare(projection, gain_vec, cosine, sine_tab):
    normed = rms_scale(projection, gain_vec)
    half_width = HD // 2
    turned = jnp.concatenate([-normed[..., half_width:], normed[..., :half_width]], axis=-1)
    return normed * cosine[:, None, :] + turned * sine_tab[:, None, :]


def visible(segments):
    tile_count = segments.shape[0] // SEGMAX
    seg_tiles = segments.reshape(tile_count, SEGMAX)
    offsets = jnp.arange(SEGMAX, dtype=jnp.int32)
    same = seg_tiles[:, :, None] == seg_tiles[:, None, :]
    return same & (offsets[:, None] >= offsets[None, :])


def tile_scores(query_tiles, key_tiles, segments):
    head_width = key_tiles.shape[-1]
    scores = jnp.einsum(
        "tqhd,tkd->thqk", query_tiles, key_tiles, preferred_element_type=jnp.float32
    ) * head_width ** (-0.5)
    return jnp.where(visible(segments)[:, None], scores, NEG_LARGE)


def attend(query_ready, key_ready, value_b, segments):
    row_count, head_count, head_width = query_ready.shape
    tile_count = row_count // SEGMAX
    query_tiles = query_ready.reshape(tile_count, SEGMAX, head_count, head_width)
    key_tiles = key_ready.reshape(tile_count, SEGMAX, head_width)
    value_tiles = value_b.reshape(tile_count, SEGMAX, head_width)
    scores = tile_scores(query_tiles, key_tiles, segments)
    row_max = jnp.max(scores, axis=-1, keepdims=True)
    row_total = jnp.sum(jnp.exp(scores - row_max), axis=-1, keepdims=True)
    log_total = row_max + jnp.log(row_total)
    probs = jnp.exp(scores - log_total).astype(jnp.bfloat16)
    attended = jnp.einsum("thqk,tkd->tqhd", probs, value_tiles, preferred_element_type=jnp.float32)
    return (attended.reshape(row_count, head_count * head_width).astype(jnp.bfloat16), log_total)


def attend_back(query_ready, key_ready, value_b, segments, log_total, d_attended):
    row_count, head_count, head_width = query_ready.shape
    tile_count = row_count // SEGMAX
    query_tiles = query_ready.reshape(tile_count, SEGMAX, head_count, head_width)
    key_tiles = key_ready.reshape(tile_count, SEGMAX, head_width)
    value_tiles = value_b.reshape(tile_count, SEGMAX, head_width)
    grad_tiles = d_attended.reshape(tile_count, SEGMAX, head_count, head_width)
    scores = tile_scores(query_tiles, key_tiles, segments)
    prob_vals = jnp.exp(scores - log_total)
    prob_b = prob_vals.astype(jnp.bfloat16)
    d_value = jnp.einsum(
        "thqk,tqhd->tkd", prob_b, grad_tiles, preferred_element_type=jnp.float32
    ).reshape(row_count, head_width)
    d_probs = jnp.einsum(
        "tqhd,tkd->thqk", grad_tiles, value_tiles, preferred_element_type=jnp.float32
    )
    row_delta = jnp.sum(prob_vals * d_probs, axis=-1, keepdims=True)
    d_scores = (prob_vals * (d_probs - row_delta) * head_width ** (-0.5)).astype(jnp.bfloat16)
    d_query = jnp.einsum(
        "thqk,tkd->tqhd", d_scores, key_tiles, preferred_element_type=jnp.float32
    ).reshape(row_count, head_count, head_width)
    d_key = jnp.einsum(
        "thqk,tqhd->tkd", d_scores, query_tiles, preferred_element_type=jnp.float32
    ).reshape(row_count, head_width)
    return (d_query, d_key, d_value)


def local(
    inputs,
    segments,
    w_query,
    w_key,
    w_value,
    w_out,
    g_in,
    g_attn,
    g_query,
    g_key,
    w_gate,
    w_up,
    w_down,
    g_pre,
    g_post,
    cotangent,
):
    attn_set = (
        lax.all_gather(w_query, "dp", axis=0, tiled=True),
        lax.all_gather(w_key, "dp", axis=0, tiled=True),
        lax.all_gather(w_value, "dp", axis=0, tiled=True),
        lax.all_gather(w_out, "dp", axis=1, tiled=True),
        lax.all_gather(g_in, "dp", axis=0, tiled=True),
        lax.all_gather(g_attn, "dp", axis=0, tiled=True),
    )
    wq_full, wk_full, wv_full, wo_full, gin_full, gattn_full = attn_set
    gain_in = gin_full.astype(jnp.float32)
    gain_attn = gattn_full.astype(jnp.float32)
    gain_query = g_query.astype(jnp.float32)
    gain_key = g_key.astype(jnp.float32)
    cosine, sine_tab = rotary_tables(segments)
    inputs_f = inputs.astype(jnp.float32)
    normed_shard = rms_scale(inputs_f, gain_in).astype(jnp.bfloat16)
    normed_in = lax.all_gather(normed_shard, "tensor", axis=0, tiled=True)
    row_count = normed_in.shape[0]
    head_count = wq_full.shape[1] // HD
    key_proj = plain_product(normed_in, wk_full)
    value_b = plain_product(normed_in, wv_full).astype(jnp.bfloat16)
    key_ready = prepare(key_proj[:, None, :], gain_key, cosine, sine_tab)[:, 0, :].astype(
        jnp.bfloat16
    )
    query_proj = plain_product(normed_in, wq_full).reshape(row_count, head_count, HD)
    query_ready = prepare(query_proj, gain_query, cosine, sine_tab).astype(jnp.bfloat16)
    attended, log_total = attend(query_ready, key_ready, value_b, segments)
    projected = lax.psum_scatter(
        plain_product(attended, wo_full), "tensor", scatter_dimension=0, tiled=True
    )
    residual_mid = inputs_f + rms_scale(projected, gain_attn)
    ffn_set = (
        lax.all_gather(w_gate, "dp", axis=0, tiled=True),
        lax.all_gather(w_up, "dp", axis=0, tiled=True),
        lax.all_gather(w_down, "dp", axis=1, tiled=True),
        lax.all_gather(g_pre, "dp", axis=0, tiled=True),
        lax.all_gather(g_post, "dp", axis=0, tiled=True),
    )
    wg_full, wu_full, wd_full, gpre_full, gpost_full = ffn_set
    gain_pre = gpre_full.astype(jnp.float32)
    gain_post = gpost_full.astype(jnp.float32)
    normed_mid = lax.all_gather(
        rms_scale(residual_mid, gain_pre).astype(jnp.bfloat16), "tensor", axis=0, tiled=True
    )
    gate_proj = plain_product(normed_mid, wg_full)
    up_proj = plain_product(normed_mid, wu_full)
    hidden = gelu_product(gate_proj, up_proj).astype(jnp.bfloat16)
    feed = lax.psum_scatter(
        plain_product(hidden, wd_full), "tensor", scatter_dimension=0, tiled=True
    )
    output = (residual_mid + rms_scale(feed, gain_post)).astype(jnp.bfloat16)
    wg_back, wu_back, wd_back = (
        lax.all_gather(w_gate, "dp", axis=0, tiled=True),
        lax.all_gather(w_up, "dp", axis=0, tiled=True),
        lax.all_gather(w_down, "dp", axis=1, tiled=True),
    )
    grad_output = cotangent.astype(jnp.float32)
    d_feed_f, grad_g_post = jax.vjp(rms_scale, feed, gain_post)[1](grad_output)
    d_feed = lax.all_gather(d_feed_f.astype(jnp.bfloat16), "tensor", axis=0, tiled=True)
    grad_down = rows_product(hidden, d_feed)
    d_hidden = cols_product(d_feed, wd_back)
    d_gate_f, d_up_f = jax.vjp(gelu_product, gate_proj, up_proj)[1](d_hidden)
    d_gate = d_gate_f.astype(jnp.bfloat16)
    d_up = d_up_f.astype(jnp.bfloat16)
    grad_gate = rows_product(normed_mid, d_gate)
    grad_up = rows_product(normed_mid, d_up)
    d_normed_mid = lax.psum_scatter(
        cols_product(d_gate, wg_back) + cols_product(d_up, wu_back),
        "tensor",
        scatter_dimension=0,
        tiled=True,
    )
    d_mid_n, grad_g_pre = jax.vjp(rms_scale, residual_mid, gain_pre)[1](d_normed_mid)
    d_mid = grad_output + d_mid_n
    d_proj_f, grad_g_attn = jax.vjp(rms_scale, projected, gain_attn)[1](d_mid)
    wq_back, wk_back, wv_back, wo_back = (
        lax.all_gather(w_query, "dp", axis=0, tiled=True),
        lax.all_gather(w_key, "dp", axis=0, tiled=True),
        lax.all_gather(w_value, "dp", axis=0, tiled=True),
        lax.all_gather(w_out, "dp", axis=1, tiled=True),
    )
    d_proj = lax.all_gather(d_proj_f.astype(jnp.bfloat16), "tensor", axis=0, tiled=True)
    grad_out = rows_product(attended, d_proj)
    d_attended = cols_product(d_proj, wo_back).astype(jnp.bfloat16)
    d_query_ready, d_key_ready, d_value_f = attend_back(
        query_ready, key_ready, value_b, segments, log_total, d_attended
    )
    rotate_fn = partial(prepare, cosine=cosine, sine_tab=sine_tab)
    d_query_f, grad_g_query = jax.vjp(rotate_fn, query_proj, gain_query)[1](d_query_ready)
    d_key_f, grad_g_key = jax.vjp(rotate_fn, key_proj[:, None, :], gain_key)[1](
        d_key_ready[:, None, :]
    )
    d_query = d_query_f.reshape(row_count, head_count * HD).astype(jnp.bfloat16)
    d_key = d_key_f[:, 0, :].astype(jnp.bfloat16)
    d_value = d_value_f.astype(jnp.bfloat16)
    grad_query = rows_product(normed_in, d_query)
    grad_key = rows_product(normed_in, d_key)
    grad_value = rows_product(normed_in, d_value)
    d_normed_terms = (
        cols_product(d_query, wq_back)
        + cols_product(d_key, wk_back)
        + cols_product(d_value, wv_back)
    )
    d_normed_in = lax.psum_scatter(
        d_normed_terms.astype(jnp.bfloat16), "tensor", scatter_dimension=0, tiled=True
    ).astype(jnp.float32)
    d_in_n, grad_g_in = jax.vjp(rms_scale, inputs_f, gain_in)[1](d_normed_in)
    d_inputs = (d_mid + d_in_n).astype(jnp.bfloat16)
    split_grads = (
        lax.psum_scatter(
            grad_query.astype(jnp.bfloat16), "dp", scatter_dimension=0, tiled=True
        ).astype(jnp.float32),
        lax.psum_scatter(
            grad_out.astype(jnp.bfloat16), "dp", scatter_dimension=1, tiled=True
        ).astype(jnp.float32),
        lax.psum_scatter(
            grad_gate.astype(jnp.bfloat16), "dp", scatter_dimension=0, tiled=True
        ).astype(jnp.float32),
        lax.psum_scatter(
            grad_up.astype(jnp.bfloat16), "dp", scatter_dimension=0, tiled=True
        ).astype(jnp.float32),
        lax.psum_scatter(
            grad_down.astype(jnp.bfloat16), "dp", scatter_dimension=1, tiled=True
        ).astype(jnp.float32),
    )
    shared = (
        lax.psum_scatter(grad_key, ("dp", "tensor"), scatter_dimension=0, tiled=True),
        lax.psum_scatter(grad_value, ("dp", "tensor"), scatter_dimension=0, tiled=True),
        lax.psum_scatter(grad_g_in, ("dp", "tensor"), scatter_dimension=0, tiled=True),
        lax.psum_scatter(grad_g_attn, ("dp", "tensor"), scatter_dimension=0, tiled=True),
        lax.psum_scatter(grad_g_pre, ("dp", "tensor"), scatter_dimension=0, tiled=True),
        lax.psum_scatter(grad_g_post, ("dp", "tensor"), scatter_dimension=0, tiled=True),
        lax.psum_scatter(grad_g_query, ("dp", "tensor"), scatter_dimension=0, tiled=True),
        lax.psum_scatter(grad_g_key, ("dp", "tensor"), scatter_dimension=0, tiled=True),
    )
    return (
        output,
        d_inputs,
        split_grads[0],
        shared[0],
        shared[1],
        split_grads[1],
        shared[2],
        shared[3],
        shared[6],
        shared[7],
        split_grads[2],
        split_grads[3],
        split_grads[4],
        shared[4],
        shared[5],
    )


def solution(mesh):
    return jax.shard_map(
        local,
        mesh=mesh,
        in_specs=(
            P(("dp", "tensor"), None),
            P("dp"),
            P("dp", "tensor"),
            P("dp", None),
            P("dp", None),
            P("tensor", "dp"),
            P("dp"),
            P("dp"),
            P(),
            P(),
            P("dp", "tensor"),
            P("dp", "tensor"),
            P("tensor", "dp"),
            P("dp"),
            P("dp"),
            P(("dp", "tensor"), None),
        ),
        out_specs=(
            P(("dp", "tensor"), None),
            P(("dp", "tensor"), None),
            P("dp", "tensor"),
            P(("dp", "tensor"), None),
            P(("dp", "tensor"), None),
            P("tensor", "dp"),
            P(("dp", "tensor")),
            P(("dp", "tensor")),
            P(("dp", "tensor")),
            P(("dp", "tensor")),
            P("dp", "tensor"),
            P("dp", "tensor"),
            P("tensor", "dp"),
            P(("dp", "tensor")),
            P(("dp", "tensor")),
        ),
        check_vma=False,
    )
```

profile of v0, /device:TPU:0, one launch (start us, length us, event | category | flops | bytes accessed | tf_op | source)
XLA Modules:
  0.0 1130.2 jit_solution(16630334409422234770)
XLA Ops:
  13.4 39.5 %all-reduce.19 = (bf16[1152]{0:T(1024)(128)(2,1)S(1)}, bf16[1152]{0:T(1024)(128)(2,1)}, bf16[1152]{0:T(1024)(128)(2,1)}, bf16[1152]{0:T(1024)(128)(2,1)}) all-reduce(bf16[1152]{0:T(1024)(128)(2,1)S(1)} %dynamic-update-slice, bf16[1152]{0:T(1024)(128)(2,1)S(1)} %dynamic-update-slice.1, ...), channel_id=1, replica_groups=mesh['dp'=8,'tensor'=4] {'dp'}, use_global_device_ids=true, to_apply=%add.4 | all-reduce | flops 4608 | bytes 18432
  62.1 31.8 %all_gather.54 = bf16[1152,256]{1,0:T(8,128)(2,1)S(1)} all-gather(bf16[144,256]{1,0:T(8,128)(2,1)S(1)} %copy-done.39), channel_id=1, replica_groups=mesh['dp'=8,'tensor'=4] {'dp'}, dimensions={0}, use_global_device_ids=true | all-gather | bytes 663552 | tf_op jit(solution)/shard_map/all_gather | solution.py:144
  93.9 31.6 %all_gather.56 = bf16[1152,256]{1,0:T(8,128)(2,1)S(1)} all-gather(bf16[144,256]{1,0:T(8,128)(2,1)S(1)} %copy-done.40), channel_id=1, replica_groups=mesh['dp'=8,'tensor'=4] {'dp'}, dimensions={0}, use_global_device_ids=true | all-gather | bytes 663552 | tf_op jit(solution)/shard_map/all_gather | solution.py:142
  125.4 31.4 %all_gather.55 = bf16[1152,256]{1,0:T(8,128)(2,1)S(1)} all-gather(bf16[144,256]{1,0:T(8,128)(2,1)S(1)} %copy-done.41), channel_id=1, replica_groups=mesh['dp'=8,'tensor'=4] {'dp'}, dimensions={0}, use_global_device_ids=true | all-gather | bytes 663552 | tf_op jit(solution)/shard_map/all_gather | solution.py:143
  156.8 33.3 %all_gather.57 = bf16[256,1152]{0,1:T(8,128)(2,1)} all-gather(bf16[256,144]{0,1:T(8,128)(2,1)S(1)} %copy-done.42), channel_id=1, replica_groups=mesh['dp'=8,'tensor'=4] {'dp'}, dimensions={1}, use_global_device_ids=true | all-gather | bytes 663552 | tf_op jit(solution)/shard_map/all_gather | solution.py:145
  207.5 44.7 %reduce-scatter.14.cloned.1.call-done = f32[256,1152]{1,0:T(8,128)} async-done(((f32[1024,1152]{1,0:T(8,128)}), f32[256,1152]{1,0:T(8,128)}) %reduce-scatter.14.cloned.1.call-update) | async-done | bytes 1179664 | tf_op jit(solution)/shard_map/reduce_scatter | solution.py:168
  258.0 20.4 %all-gather.12.cloned.1.call-done = bf16[1152,1728]{1,0:T(8,128)(2,1)} async-done(((bf16[144,1728]{1,0:T(8,128)(2,1)}), bf16[1152,1728]{1,0:T(8,128)(2,1)}) %all-gather.12.cloned.1.call-update) | async-done | bytes 3981328 | tf_op jit(solution)/shard_map/all_gather | solution.py:173
  278.4 24.6 %all-gather.10.cloned.1.call-done = bf16[1024,1152]{1,0:T(8,128)(2,1)} async-done(((bf16[256,1152]{1,0:T(8,128)(2,1)}), bf16[1024,1152]{1,0:T(8,128)(2,1)}) %all-gather.10.cloned.1.call-update) | async-done | bytes 2359312 | tf_op jit(solution)/shard_map/all_gather | solution.py:182
  303.0 10.5 fusion.75
  313.6 63.3 %all-gather.14.cloned.1.call-done = bf16[1152,1728]{1,0:T(8,128)(2,1)} async-done(((bf16[144,1728]{1,0:T(8,128)(2,1)}), bf16[1152,1728]{1,0:T(8,128)(2,1)}) %all-gather.14.cloned.1.call-update) | async-done | bytes 3981328 | tf_op jit(solution)/shard_map/all_gather | solution.py:174
  376.8 12.7 %multiply_convert_fusion.1 = (bf16[1024,1728]{0,1:T(8,128)(2,1)}, f32[1024,1728]{0,1:T(8,128)}) fusion(f32[1024,1728]{0,1:T(8,128)} %fusion.75, bf16[1024,1152]{1,0:T(8,128)(2,1)} %all-gather.10.cloned.1.call-done, bf16[1152,1728]{1,0:T(8,128)(2,1)} %all-gather.14.cloned.1.call-done), kind=kOutput, calls=%fused_computation.13 | convolution fusion | flops 4094558208 | bytes 24035328 | tf_op jit(solution)/shard_map/dot_general | solution.py:39
  389.5 59.9 %all-gather.16.cloned.1.call-done = bf16[1728,1152]{0,1:T(8,128)(2,1)} async-done(((bf16[1728,144]{0,1:T(8,128)(2,1)}), bf16[1728,1152]{0,1:T(8,128)(2,1)}) %all-gather.16.cloned.1.call-update) | async-done | bytes 3981328 | tf_op jit(solution)/shard_map/all_gather | solution.py:175
  449.4 10.4 fusion.76
  460.5 46.1 %reduce-scatter.16.cloned.1.call-done = f32[256,1152]{1,0:T(8,128)} async-done(((f32[1024,1152]{1,0:T(8,128)}), f32[256,1152]{1,0:T(8,128)}) %reduce-scatter.16.cloned.1.call-update) | async-done | bytes 1179664 | tf_op jit(solution)/shard_map/reduce_scatter | solution.py:188
  511.7 24.1 %all-gather.18.cloned.1.call-done = bf16[1024,1152]{1,0:T(8,128)(2,1)} async-done(((bf16[256,1152]{1,0:T(8,128)(2,1)}), bf16[1024,1152]{1,0:T(8,128)(2,1)}) %all-gather.18.cloned.1.call-update) | async-done | bytes 2359312 | tf_op jit(solution)/shard_map/all_gather | solution.py:199
  535.8 18.0 %multiply_convert_fusion = (bf16[1024,1728]{0,1:T(8,128)(2,1)}, bf16[1024,1728]{0,1:T(8,128)(2,1)}) fusion(f32[1024,1728]{0,1:T(8,128)} %fusion.75, f32[1024,1728]{0,1:T(8,128)} %get-tuple-element.76, bf16[1024,1152]{1,0:T(8,128)(2,1)} %all-gather.18.cloned.1.call-done, bf16[1728,1152]{0,1:T(8,128)(2,1)} %all-gather.16.cloned.1.call-done), kind=kOutput, calls=%fused_computation.12 | convolution fusion | flops 4119330816 | bytes 27574272 | tf_op jit(solution)/shard_map/dot_general | solution.py:33
  568.1 47.9 %reduce-scatter.18.cloned.1.call-done = f32[256,1152]{1,0:T(8,128)} async-done(((f32[1024,1152]{1,0:T(8,128)}), f32[256,1152]{1,0:T(8,128)}) %reduce-scatter.18.cloned.1.call-update) | async-done | bytes 1179664 | tf_op jit(solution)/shard_map/reduce_scatter | solution.py:207
  689.7 93.5 %fusion.68 = (f32[40,256]{1,0:T(8,128)S(1)}, f32[40,256]{1,0:T(8,128)S(1)}) fusion(f32[1152,256]{1,0:T(8,128)S(1)} %fusion.80, f32[1152,256]{1,0:T(8,128)} %fusion.81), kind=kCustom, calls=%all-reduce-scatter.2 | all-reduce-scatter fusion | flops 655361 | bytes 2441216
  805.5 12.8 %reduce-scatter.28.cloned.1.call-done = bf16[144,1728]{1,0:T(8,128)(2,1)} async-done(((bf16[1152,1728]{1,0:T(8,128)(2,1)}), bf16[144,1728]{1,0:T(8,128)(2,1)}) %reduce-scatter.28.cloned.1.call-update) | async-done | bytes 497680 | tf_op jit(solution)/shard_map/reduce_scatter | solution.py:259
  820.4 89.3 %reduce-scatter.30.cloned.1.call-done = bf16[1728,144]{0,1:T(8,128)(2,1)} async-done(((bf16[1728,1152]{0,1:T(8,128)(2,1)}), bf16[1728,144]{0,1:T(8,128)(2,1)}) %reduce-scatter.30.cloned.1.call-update) | async-done | bytes 497680 | tf_op jit(solution)/shard_map/reduce_scatter | solution.py:262
  914.1 61.7 %reduce-scatter.22.cloned.1.call-done = bf16[144,256]{1,0:T(8,128)(2,1)} async-done(((bf16[1152,256]{1,0:T(8,128)(2,1)}), bf16[144,256]{1,0:T(8,128)(2,1)}) %reduce-scatter.22.cloned.1.call-update) | async-done | bytes 73744 | tf_op jit(solution)/shard_map/reduce_scatter | solution.py:250
  977.3 63.6 %reduce-scatter.24.cloned.1.call-done = bf16[256,144]{0,1:T(8,128)(2,1)} async-done(((bf16[256,1152]{0,1:T(8,128)(2,1)}), bf16[256,144]{0,1:T(8,128)(2,1)}) %reduce-scatter.24.cloned.1.call-update) | async-done | bytes 73744 | tf_op jit(solution)/shard_map/reduce_scatter | solution.py:253
  1042.5 32.6 %reduce-scatter.20.cloned.1.call-done = bf16[256,1152]{1,0:T(8,128)(2,1)} async-done(((bf16[1024,1152]{1,0:T(8,128)(2,1)}), bf16[256,1152]{1,0:T(8,128)(2,1)}) %reduce-scatter.20.cloned.1.call-update) | async-done | bytes 589840 | tf_op jit(solution)/shard_map/reduce_scatter | solution.py:244
  1076.7 39.9 %all-reduce.18 = (f32[1152]{0:T(1024)S(1)}, f32[1152]{0:T(1024)S(1)}, f32[256]{0:T(256)S(1)}, f32[256]{0:T(256)S(1)}, f32[1152]{0:T(1024)S(1)}, /*index=5*/f32[1152]{0:T(1024)S(1)}) all-reduce(f32[1152]{0:T(1024)S(1)} %get-tuple-element.25, ...), channel_id=10, replica_groups=mesh['dp'=8,'tensor'=4] {'dp','tensor'}, use_global_device_ids=true, to_apply=%region_26.27.clone | all-reduce | flops 5120 | bytes 40960
  (286 shorter events, 169.2 us)
Async XLA Ops:
  8.0 182.1 %all-gather.8.cloned.1.call-start = ((), (), s32[]{:S(2)}) async-start(), calls=%async_computation.9 | async-start | bytes 2949120 | tf_op jit(solution)/shard_map/all_gather | solution.py:157
  57.4 194.7 %reduce-scatter.14.cloned.1.call-start = ((), (), s32[]{:S(2)}) async-start(), calls=%async_computation.10 | async-start | bytes 5898240 | tf_op jit(solution)/shard_map/reduce_scatter | solution.py:168
  206.8 71.7 %all-gather.12.cloned.1.call-start = ((), (), s32[]{:S(2)}) async-start(), calls=%async_computation.12 | async-start | bytes 4644864 | tf_op jit(solution)/shard_map/all_gather | solution.py:173
  207.4 95.7 %all-gather.10.cloned.1.call-start = ((), (), s32[]{:S(2)}) async-start(), calls=%async_computation.11 | async-start | bytes 2949120 | tf_op jit(solution)/shard_map/all_gather | solution.py:182
  256.5 120.4 %all-gather.14.cloned.1.call-start = ((), (), s32[]{:S(2)}) async-start(), calls=%async_computation.13 | async-start | bytes 4644864 | tf_op jit(solution)/shard_map/all_gather | solution.py:174
  257.0 192.4 %all-gather.16.cloned.1.call-start = ((), (), s32[]{:S(2)}) async-start(), calls=%async_computation.14 | async-start | bytes 4644864 | tf_op jit(solution)/shard_map/all_gather | solution.py:175
  257.8 248.8 %reduce-scatter.16.cloned.1.call-start = ((), (), s32[]{:S(2)}) async-start(), calls=%async_computation.15 | async-start | bytes 5898240 | tf_op jit(solution)/shard_map/reduce_scatter | solution.py:188
  459.8 76.0 %all-gather.18.cloned.1.call-start = ((), (), s32[]{:S(2)}) async-start(), calls=%async_computation.16 | async-start | bytes 2949120 | tf_op jit(solution)/shard_map/all_gather | solution.py:199
  511.6 104.4 %reduce-scatter.18.cloned.1.call-start = ((), (), s32[]{:S(2)}) async-start(), calls=%async_computation.17 | async-start | bytes 5898240 | tf_op jit(solution)/shard_map/reduce_scatter | solution.py:207
  568.1 82.3 %all-gather.20.cloned.1.call-start = ((), (), s32[]{:S(2)}) async-start(), calls=%async_computation.18 | async-start | bytes 2949120 | tf_op jit(solution)/shard_map/all_gather | solution.py:222
  621.9 181.5 %reduce-scatter.26.cloned.1.call-start = ((), (), s32[]{:S(2)}) async-start(), calls=%async_computation.22 | async-start | bytes 4644864 | tf_op jit(solution)/shard_map/reduce_scatter | solution.py:256
  631.2 187.1 %reduce-scatter.28.cloned.1.call-start = ((), (), s32[]{:S(2)}) async-start(), calls=%async_computation.23 | async-start | bytes 4644864 | tf_op jit(solution)/shard_map/reduce_scatter | solution.py:259
  640.7 268.9 %reduce-scatter.30.cloned.1.call-start = ((), (), s32[]{:S(2)}) async-start(), calls=%async_computation.24 | async-start | bytes 4644864 | tf_op jit(solution)/shard_map/reduce_scatter | solution.py:262
  650.0 325.8 %reduce-scatter.22.cloned.1.call-start = ((), (), s32[]{:S(2)}) async-start(), calls=%async_computation.20 | async-start | bytes 663552 | tf_op jit(solution)/shard_map/reduce_scatter | solution.py:250
  668.6 372.4 %reduce-scatter.24.cloned.1.call-start = ((), (), s32[]{:S(2)}) async-start(), calls=%async_computation.21 | async-start | bytes 663552 | tf_op jit(solution)/shard_map/reduce_scatter | solution.py:253
  677.2 397.8 %reduce-scatter.20.cloned.1.call-start = ((), (), s32[]{:S(2)}) async-start(), calls=%async_computation.19 | async-start | bytes 2949120 | tf_op jit(solution)/shard_map/reduce_scatter | solution.py:244
  783.2 12.9 %collective-permute-start.2 = (f32[40,256]{1,0:T(8,128)S(1)}, f32[40,256]{1,0:T(8,128)S(1)}, u32[]{:S(2)}, u32[]{:S(2)}) collective-permute-start(f32[40,256]{1,0:T(8,128)S(1)} %get-tuple-element.39), channel_id=1, source_target_pairs={{0,3},{1,4},{2,5},{3,6},{4,7},{5,8},{6,9},{7,10},{8,11},{9,12},{10... | collective-permute-start | bytes 122888
  784.5 14.8 %collective-permute-start.1 = (f32[40,256]{1,0:T(8,128)S(1)}, f32[40,256]{1,0:T(8,128)S(1)}, u32[]{:S(2)}, u32[]{:S(2)}) collective-permute-start(f32[40,256]{1,0:T(8,128)S(1)} %get-tuple-element.39), channel_id=1, source_target_pairs={{0,2},{1,3},{2,4},{3,5},{4,6},{5,7},{6,8},{7,9},{8,10},{9,11},{10,... | collective-permute-start | bytes 122888
  785.8 4.5 collective-permute-start.3
  787.1 124.6 %collective-permute-start = (f32[40,256]{1,0:T(8,128)S(1)}, f32[40,256]{1,0:T(8,128)S(1)}, u32[]{:S(2)}, u32[]{:S(2)}) collective-permute-start(f32[40,256]{1,0:T(8,128)S(1)} %get-tuple-element.39), channel_id=1, source_target_pairs={{0,1},{1,2},{2,3},{3,4},{4,5},{5,6},{6,7},{7,8},{8,9},{9,10},{10,1... | collective-permute-start | bytes 122888
  788.4 123.8 %collective-permute-start.6 = (f32[40,256]{1,0:T(8,128)S(1)}, f32[40,256]{1,0:T(8,128)S(1)}, u32[]{:S(2)}, u32[]{:S(2)}) collective-permute-start(f32[40,256]{1,0:T(8,128)S(1)} %get-tuple-element.40), channel_id=1, source_target_pairs={{0,3},{1,4},{2,5},{3,6},{4,7},{5,8},{6,9},{7,10},{8,11},{9,12},{10... | collective-permute-start | bytes 122888
  790.4 121.9 %collective-permute-start.5 = (f32[40,256]{1,0:T(8,128)S(1)}, f32[40,256]{1,0:T(8,128)S(1)}, u32[]{:S(2)}, u32[]{:S(2)}) collective-permute-start(f32[40,256]{1,0:T(8,128)S(1)} %get-tuple-element.40), channel_id=1, source_target_pairs={{0,2},{1,3},{2,4},{3,5},{4,6},{5,7},{6,8},{7,9},{8,10},{9,11},{10,... | collective-permute-start | bytes 122888
  796.2 116.1 %collective-permute-start.4 = (f32[40,256]{1,0:T(8,128)S(1)}, f32[40,256]{1,0:T(8,128)S(1)}, u32[]{:S(2)}, u32[]{:S(2)}) collective-permute-start(f32[40,256]{1,0:T(8,128)S(1)} %get-tuple-element.40), channel_id=1, source_target_pairs={{0,1},{1,2},{2,3},{3,4},{4,5},{5,6},{6,7},{7,8},{8,9},{9,10},{10,1... | collective-permute-start | bytes 122888
  799.3 112.9 %collective-permute-start.7 = (f32[4,256]{1,0:T(4,128)S(1)}, f32[4,256]{1,0:T(4,128)S(1)}, u32[]{:S(2)}, u32[]{:S(2)}) collective-permute-start(f32[4,256]{1,0:T(4,128)S(1)} %slice.35), channel_id=1, source_target_pairs={{0,4},{1,5},{2,6},{3,7},{4,8},{5,9},{6,10},{7,11},{8,12},{9,13},{1... | collective-permute-start | bytes 12296
  (65 other events, 2067.8 us)
Sparse Core Ops, SparseCore 0:
  57.5 21.2 all-gather.7
  206.9 45.2 reduce-scatter.13
  459.9 46.5 reduce-scatter.15
  511.7 24.0 all-gather.17
  622.0 24.0 all-gather.19
Sparse Core Ops, SparseCore 1:
  209.5 68.9 all-gather.11
  280.5 22.5 all-gather.9
  305.1 71.7 all-gather.13
  379.0 70.3 all-gather.15
  568.2 47.8 reduce-scatter.17
  631.3 90.5 reduce-scatter.25
  725.2 93.0 reduce-scatter.27
  821.7 87.8 reduce-scatter.29
  913.4 62.4 reduce-scatter.21
  979.1 61.8 reduce-scatter.23
  1043.3 31.7 reduce-scatter.19
where the time goes:
time: 1140 us; the launch traced here: 1130 us
  waiting for transfers between devices  593 us (52%)
  blocking collectives  301 us (26%)
  matrix products  130 us (11%)
  other arithmetic  39.8 us (3%)
  local copies, waits for them, and re-layouts  28.1 us (2%)
  starting transfers between devices  21.4 us (2%)
  between operations  17.6 us (2%)
    unnamed x3, blocking collectives  173 us
    reduce_scatter x1, waiting for transfers between devices, local(): lax.psum_scatter(grad_down.astype(jnp.bfloat16), 'dp', scatter_dimension=...  89.3 us
    reduce_scatter x1, waiting for transfers between devices, local(): lax.psum_scatter(grad_out.astype(jnp.bfloat16), 'dp', scatter_dimension=1...  63.6 us
    all_gather x1, waiting for transfers between devices, local(): lax.all_gather(w_up, 'dp', axis=0, tiled=True)  63.3 us
    reduce_scatter x1, waiting for transfers between devices, local(): lax.psum_scatter(grad_query.astype(jnp.bfloat16), 'dp', scatter_dimension...  61.7 us
    all_gather x1, waiting for transfers between devices, local(): lax.all_gather(w_down, 'dp', axis=1, tiled=True)  59.9 us
    reduce_scatter x1, waiting for transfers between devices, local(): lax.psum_scatter(cols_product(d_gate, wg_back) + cols_product(d_up, wu_ba...  47.9 us
    reduce_scatter x1, waiting for transfers between devices, local(): lax.psum_scatter(plain_product(hidden, wd_full), 'tensor', scatter_dimens...  46.1 us
  transfers between devices with their start and end apart: 24, of which 13 were waited for; matrix products, arithmetic and copies ran while one was open for 17% of the time, Pallas kernels for 0%

commit v1 on v0

--- a/solution.py
+++ b/solution.py
@@ -1,12 +1,274 @@
+import functools
 from functools import partial
 
 import jax
 import jax.numpy as jnp
 from jax import lax
+from jax.experimental import pallas as pl
+from jax.experimental.pallas import tpu as pltpu
 from jax.sharding import PartitionSpec as P
 
 HD = 256
 SEGMAX = 512
+MESH = pl.DeviceIdType.MESH
+BF = jnp.bfloat16
+F32 = jnp.float32
+
+
+def ring_pos(dev, n):
+    return (1 - dev % 2) * (dev // 2) + (dev % 2) * (n - 1 - dev // 2)
+
+
+def ring_dev(pos, n):
+    high = pos // (n // 2)
+    return (1 - high) * (2 * pos) + high * (2 * (n - 1 - pos) + 1)
+
+
+def barrier(peers):
+    sem = pltpu.get_barrier_semaphore()
+    for peer in peers:
+        pl.semaphore_signal(sem, inc=1, device_id=peer, device_id_type=MESH)
+    pl.semaphore_wait(sem, len(peers))
+
+
+def reach(bias, way, n):
+    return n // 2 if bias == way else n // 2 - 1
+
+
+class Ring:
+    def __init__(self, n, parts, send_sem, recv_sem, land=None):
+        self.n, self.parts, self.land = n, parts, land
+        self.send_sem, self.recv_sem = send_sem, recv_sem
+        self.me = lax.axis_index("dp")
+        self.pos = ring_pos(self.me, n)
+        self.peer = [{"dp": self.dev(1)}, {"dp": self.dev(-1)}]
+
+    def dev(self, offset):
+        return ring_dev((self.pos + (offset + self.n) % self.n) % self.n, self.n)
+
+    def reach(self, part, way):
+        return reach(part % 2, way, self.n)
+
+    def gather(self, part, way, hop, ahead):
+        away = hop - 1 if ahead else hop
+        block = self.parts[part](self.dev(-away if way == 0 else away))
+        return pltpu.make_async_remote_copy(
+            block,
+            block,
+            self.send_sem.at[part, way, hop - 1],
+            self.recv_sem.at[part, way, hop - 1],
+            device_id=self.peer[way],
+            device_id_type=MESH,
+        )
+
+    def gather_step(self, part, way, hop):
+        if hop > 1:
+            self.gather(part, way, hop - 1, False).wait_recv()
+        if hop <= self.reach(part, way):
+            self.gather(part, way, hop, True).start()
+
+    def gather_sends_done(self, part):
+        for way in range(2):
+            for hop in range(1, self.reach(part, way) + 1):
+                self.gather(part, way, hop, True).wait_send()
+
+    def target(self, part, way, hop):
+        away = self.reach(part, way) - hop + 1
+        return self.dev(away if way == 0 else -away)
+
+    def slot(self, part, way, hop):
+        return self.land(part, hop - 1 + (self.reach(part, 0) if way else 0))
+
+    def reduce(self, part, way, hop):
+        return pltpu.make_async_remote_copy(
+            self.parts[part](self.target(part, way, hop)),
+            self.slot(part, way, hop),
+            self.send_sem.at[part, way, hop - 1],
+            self.recv_sem.at[part, way, hop - 1],
+            device_id=self.peer[way],
+            device_id_type=MESH,
+        )
+
+    def reduce_step(self, part, way, hop):
+        if hop > self.reach(part, way):
+            return
+        if hop > 1:
+            self.reduce(part, way, hop - 1).wait_recv()
+            own = self.parts[part](self.target(part, way, hop))
+            came = self.slot(part, way, hop - 1)
+            own[...] = (own[...].astype(F32) + came[...].astype(F32)).astype(BF)
+        self.reduce(part, way, hop).start()
+
+    def reduce_end(self, part):
+        total = self.parts[part](self.me)[...].astype(F32)
+        for way in range(2):
+            last = self.reach(part, way)
+            self.reduce(part, way, last).wait_recv()
+            total = total + self.slot(part, way, last)[...].astype(F32)
+        return total
+
+    def reduce_sends_done(self, part):
+        for way in range(2):
+            for hop in range(1, self.reach(part, way) + 1):
+                self.reduce(part, way, hop).wait_send()
+
+
+def part_views(attn, ffn, attn_cut, ffn_cut):
+    views = []
+    for low, high in attn_cut:
+        views.append(lambda b, low=low, high=high: attn.at[b, :, pl.ds(low, high - low)])
+    for chunk in range(ffn.shape[0]):
+        for low, high in ffn_cut:
+            views.append(
+                lambda b, c=chunk, low=low, high=high: ffn.at[c, b, :, pl.ds(low, high - low)]
+            )
+    return views
+
+
+def halves(cols, step=128):
+    mid = cols // 2 // step * step
+    return ((0, mid), (mid, cols))
+
+
+def gather_kernel(n, attn_ref, ffn_ref, attn_out, ffn_out, local_sem, send_sem, recv_sem):
+    parts = part_views(attn_out, ffn_out, halves(attn_ref.shape[-1]), halves(ffn_ref.shape[-1]))
+    ring = Ring(n, parts, send_sem, recv_sem)
+    mine = [
+        pltpu.make_async_copy(attn_ref, attn_out.at[ring.me], local_sem.at[0]),
+        pltpu.make_async_copy(ffn_ref, ffn_out.at[:, ring.me], local_sem.at[1]),
+    ]
+    for copy in mine:
+        copy.start()
+    barrier(ring.peer)
+    for copy in mine:
+        copy.wait()
+    width = 4
+    for low in range(0, len(parts), width):
+        for hop in range(1, n // 2 + 2):
+            for part in range(low, min(low + width, len(parts))):
+                for way in range(2):
+                    if hop <= ring.reach(part, way) + 1:
+                        ring.gather_step(part, way, hop)
+    for part in range(len(parts)):
+        ring.gather_sends_done(part)
+
+
+def reduce_kernel(n, attn_ref, ffn_ref, attn_out, ffn_out, attn_buf, ffn_buf, attn_land, ffn_land, local_sem, send_sem, recv_sem):
+    acut, fcut = halves(attn_ref.shape[-1]), halves(ffn_ref.shape[-1])
+    parts = part_views(attn_buf, ffn_buf, acut, fcut)
+    landing = part_views(attn_land, ffn_land, acut, fcut)
+    ring = Ring(n, parts, send_sem, recv_sem, lambda part, slot: landing[part](slot))
+    load = [
+        pltpu.make_async_copy(attn_ref, attn_buf, local_sem.at[0]),
+        pltpu.make_async_copy(ffn_ref, ffn_buf, local_sem.at[1]),
+    ]
+    for copy in load:
+        copy.start()
+    barrier(ring.peer)
+    for copy in load:
+        copy.wait()
+    width = 4
+    for low in range(0, len(parts), width):
+        for hop in range(1, n // 2 + 1):
+            for part in range(low, min(low + width, len(parts))):
+                for way in range(2):
+                    ring.reduce_step(part, way, hop)
+        for part in range(low, min(low + width, len(parts))):
+            total = ring.reduce_end(part)
+            if part < 2:
+                attn_out[:, acut[part][0] : acut[part][1]] = total
+            else:
+                cut = fcut[part % 2]
+                ffn_out[part // 2 - 1, :, cut[0] : cut[1]] = total
+    for part in range(len(parts)):
+        ring.reduce_sends_done(part)
+
+
+VMEM_LIMIT = 60 * 2**20
+
+
+def vmem_specs(count):
+    return [pl.BlockSpec(memory_space=pltpu.VMEM)] * count
+
+
+def any_specs(count):
+    return [pl.BlockSpec(memory_space=pl.ANY)] * count
+
+
+def ring_gather(n, attn, ffn):
+    chunks = ffn.shape[0]
+    sems = pltpu.SemaphoreType.DMA((2 * (chunks + 1), 2, n // 2))
+    return pl.pallas_call(
+        partial(gather_kernel, n),
+        out_shape=(
+            jax.ShapeDtypeStruct((n,) + attn.shape, BF),
+            jax.ShapeDtypeStruct((chunks, n) + ffn.shape[1:], BF),
+        ),
+        in_specs=any_specs(2),
+        out_specs=vmem_specs(2),
+        scratch_shapes=[pltpu.SemaphoreType.DMA((2,)), sems, sems],
+        compiler_params=pltpu.CompilerParams(
+            collective_id=0, has_side_effects=True, vmem_limit_bytes=VMEM_LIMIT
+        ),
+    )(attn, ffn)
+
+
+def ring_reduce(n, attn, ffn):
+    chunks, _, rows, cols = ffn.shape
+    sems = pltpu.SemaphoreType.DMA((2 * (chunks + 1), 2, n // 2))
+    return pl.pallas_call(
+        partial(reduce_kernel, n),
+        out_shape=(
+            jax.ShapeDtypeStruct(attn.shape[1:], F32),
+            jax.ShapeDtypeStruct((chunks, rows, cols), F32),
+        ),
+        in_specs=any_specs(2),
+        out_specs=vmem_specs(2),
+        scratch_shapes=[
+            pltpu.VMEM(attn.shape, BF),
+            pltpu.VMEM(ffn.shape, BF),
+            pltpu.VMEM((n - 1,) + attn.shape[1:], BF),
+            pltpu.VMEM((chunks, n - 1, rows, cols), BF),
+            pltpu.SemaphoreType.DMA((2,)),
+            sems,
+            sems,
+        ],
+        compiler_params=pltpu.CompilerParams(
+            collective_id=1, has_side_effects=True, vmem_limit_bytes=VMEM_LIMIT
+        ),
+    )(attn, ffn)
+
+
+CHUNK = 256
+
+
+def pack_rows(array, rows):
+    return jnp.pad(array, ((0, rows - array.shape[0]), (0, 0)))
+
+
+def pack_ffn(gate, up, down_t, rows):
+    width = gate.shape[1]
+    chunks = -(-width // CHUNK)
+
+    def cut(array):
+        array = jnp.pad(array, ((0, rows - array.shape[0]), (0, chunks * CHUNK - width)))
+        return array.reshape(rows, chunks, CHUNK).transpose(1, 0, 2)
+
+    return jnp.concatenate([cut(gate), cut(up), cut(down_t)], axis=2)
+
+
+def unpack_ffn(packed, width):
+    chunks, rows = packed.shape[:2]
+    out = []
+    for k in range(3):
+        piece = packed[:, :, k * CHUNK : (k + 1) * CHUNK]
+        out.append(piece.transpose(1, 0, 2).reshape(rows, chunks * CHUNK)[:, :width])
+    return out
+
+
+def pack_blocks(array, n, rows):
+    depth = array.shape[0] // n
+    return jnp.pad(array.reshape(n, depth, -1), ((0, 0), (0, rows - depth), (0, 0)))
 
 
 EPSILON = 1e-06
@@ -138,15 +400,24 @@
     g_post,
     cotangent,
 ):
-    attn_set = (
-        lax.all_gather(w_query, "dp", axis=0, tiled=True),
-        lax.all_gather(w_key, "dp", axis=0, tiled=True),
-        lax.all_gather(w_value, "dp", axis=0, tiled=True),
-        lax.all_gather(w_out, "dp", axis=1, tiled=True),
-        lax.all_gather(g_in, "dp", axis=0, tiled=True),
-        lax.all_gather(g_attn, "dp", axis=0, tiled=True),
-    )
-    wq_full, wk_full, wv_full, wo_full, gin_full, gattn_full = attn_set
+    n = lax.axis_size("dp")
+    depth = w_query.shape[0]
+    rows = -(-depth // 16) * 16
+    width = w_gate.shape[1]
+    gains = jnp.stack([g_in, g_attn, g_pre, g_post], axis=1)
+    attn_pack = jnp.concatenate(
+        [w_query, w_key, w_value, w_out.T, jnp.pad(gains, ((0, 0), (0, 124)))], axis=1
+    )
+    attn_all, ffn_all = ring_gather(
+        n, pack_rows(attn_pack, rows), pack_ffn(w_gate, w_up, w_down.T, rows)
+    )
+    attn_all = attn_all[:, :depth].reshape(n * depth, -1)
+    ffn_all = ffn_all[:, :, :depth].reshape(ffn_all.shape[0], n * depth, -1)
+    wq_full, wk_full, wv_full, wo_t = (attn_all[:, k * HD : (k + 1) * HD] for k in range(4))
+    wo_full = wo_t.T
+    gin_full, gattn_full, gpre_full, gpost_full = (attn_all[:, 4 * HD + k] for k in range(4))
+    wg_full, wu_full, wd_t = unpack_ffn(ffn_all, width)
+    wd_full = wd_t.T
     gain_in = gin_full.astype(jnp.float32)
     gain_attn = gattn_full.astype(jnp.float32)
     gain_query = g_query.astype(jnp.float32)
@@ -169,14 +440,6 @@
         plain_product(attended, wo_full), "tensor", scatter_dimension=0, tiled=True
     )
     residual_mid = inputs_f + rms_scale(projected, gain_attn)
-    ffn_set = (
-        lax.all_gather(w_gate, "dp", axis=0, tiled=True),
-        lax.all_gather(w_up, "dp", axis=0, tiled=True),
-        lax.all_gather(w_down, "dp", axis=1, tiled=True),
-        lax.all_gather(g_pre, "dp", axis=0, tiled=True),
-        lax.all_gather(g_post, "dp", axis=0, tiled=True),
-    )
-    wg_full, wu_full, wd_full, gpre_full, gpost_full = ffn_set
     gain_pre = gpre_full.astype(jnp.float32)
     gain_post = gpost_full.astype(jnp.float32)
     normed_mid = lax.all_gather(
@@ -189,15 +452,10 @@
         plain_product(hidden, wd_full), "tensor", scatter_dimension=0, tiled=True
     )
     output = (residual_mid + rms_scale(feed, gain_post)).astype(jnp.bfloat16)
-    wg_back, wu_back, wd_back = (
-        lax.all_gather(w_gate, "dp", axis=0, tiled=True),
-        lax.all_gather(w_up, "dp", axis=0, tiled=True),
-        lax.all_gather(w_down, "dp", axis=1, tiled=True),
-    )
+    wg_back, wu_back, wd_back = wg_full, wu_full, wd_full
     grad_output = cotangent.astype(jnp.float32)
     d_feed_f, grad_g_post = jax.vjp(rms_scale, feed, gain_post)[1](grad_output)
     d_feed = lax.all_gather(d_feed_f.astype(jnp.bfloat16), "tensor", axis=0, tiled=True)
-    grad_down = rows_product(hidden, d_feed)
     d_hidden = cols_product(d_feed, wd_back)
     d_gate_f, d_up_f = jax.vjp(gelu_product, gate_proj, up_proj)[1](d_hidden)
     d_gate = d_gate_f.astype(jnp.bfloat16)
@@ -213,14 +471,8 @@
     d_mid_n, grad_g_pre = jax.vjp(rms_scale, residual_mid, gain_pre)[1](d_normed_mid)
     d_mid = grad_output + d_mid_n
     d_proj_f, grad_g_attn = jax.vjp(rms_scale, projected, gain_attn)[1](d_mid)
-    wq_back, wk_back, wv_back, wo_back = (
-        lax.all_gather(w_query, "dp", axis=0, tiled=True),
-        lax.all_gather(w_key, "dp", axis=0, tiled=True),
-        lax.all_gather(w_value, "dp", axis=0, tiled=True),
-        lax.all_gather(w_out, "dp", axis=1, tiled=True),
-    )
+    wq_back, wk_back, wv_back, wo_back = wq_full, wk_full, wv_full, wo_full
     d_proj = lax.all_gather(d_proj_f.astype(jnp.bfloat16), "tensor", axis=0, tiled=True)
-    grad_out = rows_product(attended, d_proj)
     d_attended = cols_product(d_proj, wo_back).astype(jnp.bfloat16)
     d_query_ready, d_key_ready, d_value_f = attend_back(
         query_ready, key_ready, value_b, segments, log_total, d_attended
@@ -246,26 +498,28 @@
     ).astype(jnp.float32)
     d_in_n, grad_g_in = jax.vjp(rms_scale, inputs_f, gain_in)[1](d_normed_in)
     d_inputs = (d_mid + d_in_n).astype(jnp.bfloat16)
+    attn_part = jnp.concatenate(
+        [grad_query, grad_key, grad_value, rows_product(d_proj, attended)], axis=1
+    ).astype(BF)
+    attn_part = pack_blocks(attn_part, n, rows)
+    ffn_part = pack_ffn(
+        grad_gate.astype(BF), grad_up.astype(BF), rows_product(d_feed, hidden).astype(BF), n * depth
+    )
+    ffn_part = jax.vmap(lambda a: pack_blocks(a, n, rows))(ffn_part)
+    attn_sum, ffn_sum = ring_reduce(n, attn_part, ffn_part)
+    attn_sum, ffn_sum = attn_sum[:depth], ffn_sum[:, :depth]
+    sum_gate, sum_up, sum_down_t = unpack_ffn(ffn_sum, width)
     split_grads = (
-        lax.psum_scatter(
-            grad_query.astype(jnp.bfloat16), "dp", scatter_dimension=0, tiled=True
-        ).astype(jnp.float32),
-        lax.psum_scatter(
-            grad_out.astype(jnp.bfloat16), "dp", scatter_dimension=1, tiled=True
-        ).astype(jnp.float32),
-        lax.psum_scatter(
-            grad_gate.astype(jnp.bfloat16), "dp", scatter_dimension=0, tiled=True
-        ).astype(jnp.float32),
-        lax.psum_scatter(
-            grad_up.astype(jnp.bfloat16), "dp", scatter_dimension=0, tiled=True
-        ).astype(jnp.float32),
-        lax.psum_scatter(
-            grad_down.astype(jnp.bfloat16), "dp", scatter_dimension=1, tiled=True
-        ).astype(jnp.float32),
-    )
+        attn_sum[:, :HD],
+        attn_sum[:, 3 * HD : 4 * HD].T,
+        sum_gate,
+        sum_up,
+        sum_down_t.T,
+    )
+    sum_key, sum_value = attn_sum[:, HD : 2 * HD], attn_sum[:, 2 * HD : 3 * HD]
     shared = (
-        lax.psum_scatter(grad_key, ("dp", "tensor"), scatter_dimension=0, tiled=True),
-        lax.psum_scatter(grad_value, ("dp", "tensor"), scatter_dimension=0, tiled=True),
+        lax.psum_scatter(sum_key, "tensor", scatter_dimension=0, tiled=True),
+        lax.psum_scatter(sum_value, "tensor", scatter_dimension=0, tiled=True),
         lax.psum_scatter(grad_g_in, ("dp", "tensor"), scatter_dimension=0, tiled=True),
         lax.psum_scatter(grad_g_attn, ("dp", "tensor"), scatter_dimension=0, tiled=True),
         lax.psum_scatter(grad_g_pre, ("dp", "tensor"), scatter_dimension=0, tiled=True),

time: 1140 us -> 829 us (0.73)
  waiting for transfers between devices: 593 us -> 187 us
  Pallas kernels: 0 us -> 315 us
  blocking collectives: 301 us -> 48.2 us
  local copies, waits for them, and re-layouts: 28.1 us -> 102 us
  matrix products: 130 us -> 102 us
  starting transfers between devices: 21.4 us -> 5.6 us
    pallas_call x0 -> x2, Pallas kernels: none -> 315 us  [the longest x1 160 us: ring_gather(): pl.pallas_call(partial(gather_kernel, n), out_shape=(jax.ShapeDtypeStruct...]
    reduce_scatter x5 -> x0, waiting for transfers between devices: 227 us -> none  [the longest x1 89.3 us: local(): lax.psum_scatter(grad_down.astype(jnp.bfloat16), 'dp', scatter_dimension=...]
    all_gather x3 -> x0, waiting for transfers between devices: 144 us -> none  [the longest x1 63.3 us: local(): lax.all_gather(w_up, 'dp', axis=0, tiled=True)]
    all_gather x4 -> x0, blocking collectives: 128 us -> none  [the longest x1 33.3 us: local(): lax.all_gather(w_out, 'dp', axis=1, tiled=True)]
    unnamed x3 -> x2, blocking collectives: 173 us -> 48.2 us
    reduce_scatter x1, waiting for transfers between devices: 32.6 us -> 0.01 us  [local(): lax.psum_scatter(d_normed_terms.astype(jnp.bfloat16), 'tensor', scatter_d...]
    all_gather x1, waiting for transfers between devices: 24.6 us -> 0.01 us  [local(): lax.all_gather(rms_scale(residual_mid, gain_pre).astype(jnp.bfloat16), 't...]
    reshape x0 -> x7, local copies, waits for them, and re-layouts: none -> 21.5 us  [the longest x4 19.4 us: cut(): return array.reshape(rows, chunks, CHUNK).transpose(1, 0, 2)]
  transfers between devices with their start and end apart: 24 -> 10, of which waited for: 13 -> 6; matrix products, arithmetic and copies ran while one was open for 17% -> 16% of each run, Pallas kernels for 0% -> 19%
where the time goes in v1:
time: 829 us; the launch traced here: 819 us
  Pallas kernels  315 us (38%)
  waiting for transfers between devices  187 us (23%)
  local copies, waits for them, and re-layouts  102 us (12%)
  matrix products  102 us (12%)
  blocking collectives  48.2 us (6%)
  other arithmetic  42.4 us (5%)
  between operations  16.2 us (2%)
    pallas_call x1, Pallas kernels, ring_gather(): pl.pallas_call(partial(gather_kernel, n), out_shape=(jax.ShapeDtypeStruct...  160 us
    pallas_call x1, Pallas kernels, ring_reduce(): pl.pallas_call(partial(reduce_kernel, n), out_shape=(jax.ShapeDtypeStruct...  155 us
    unnamed x2, blocking collectives  48.2 us
    reduce_scatter x1, waiting for transfers between devices, local(): lax.psum_scatter(cols_product(d_gate, wg_back) + cols_product(d_up, wu_ba...  47.9 us
    reduce_scatter x1, waiting for transfers between devices, local(): lax.psum_scatter(plain_product(hidden, wd_full), 'tensor', scatter_dimens...  46.9 us
    reduce_scatter x1, waiting for transfers between devices, local(): lax.psum_scatter(plain_product(attended, wo_full), 'tensor', scatter_dime...  46.8 us
    unnamed x139, local copies, waits for them, and re-layouts  41.7 us
    dot_general x7, matrix products, cols_product(): lax.dot_general(left, right, (((1,), (1,)), ((), ())), preferred_element_...  33.8 us
  transfers between devices with their start and end apart: 10, of which 6 were waited for; matrix products, arithmetic and copies ran while one was open for 16% of the time, Pallas kernels for 19%

profile of v1, /device:TPU:0, one launch (start us, length us, event | category | flops | bytes accessed | tf_op | source)
XLA Modules:
  0.0 819.1 jit_solution(12137132160310910817)
XLA Ops:
  14.8 159.9 %shard_map.271 = (bf16[8,144,1152]{2,1,0:T(8,128)(2,1)}, bf16[7,8,144,768]{3,2,1,0:T(8,128)(2,1)}) custom-call(bf16[144,1152]{1,0:T(8,128)(2,1)} %copy-done.35, bf16[7,144,768]{2,1,0:T(8,128)(2,1)} %pad_maximum_fusion.2.ffn_ref), custom_call_target="tpu_custom_call" | custom-call | tf_op jit(solution)/shard_map/pallas_call | solution.py:201
  182.9 19.2 %all-gather.5.cloned.1.call-done = bf16[1024,1152]{1,0:T(8,128)(2,1)} async-done(((bf16[256,1152]{1,0:T(8,128)(2,1)}), bf16[1024,1152]{1,0:T(8,128)(2,1)}) %all-gather.5.cloned.1.call-update) | async-done | bytes 2359312 | tf_op jit(solution)/shard_map/all_gather | solution.py:428
  220.4 46.8 %reduce-scatter.9.cloned.1.call-done = f32[256,1152]{1,0:T(8,128)} async-done(((f32[1024,1152]{1,0:T(8,128)}), f32[256,1152]{1,0:T(8,128)}) %reduce-scatter.9.cloned.1.call-update) | async-done | bytes 1179664 | tf_op jit(solution)/shard_map/reduce_scatter | solution.py:439
  271.7 8.5 %fusion.96 = (bf16[7,1152,256]{2,1,0:T(8,128)(2,1)}, bf16[7,1152,256]{2,1,0:T(8,128)(2,1)}, bf16[7,1152,256]{2,1,0:T(8,128)(2,1)}) fusion(bf16[7,1152,768]{2,1,0:T(8,128)(2,1)} %bitcast.213), kind=kLoop, calls=%fused_computation.202 | loop fusion | bytes 24772608 | tf_op jit(solution)/shard_map/slice | solution.py:264
  280.2 6.5 copy.103
  286.6 6.5 copy.104
  293.1 6.5 copy.105
  299.6 7.4 fusion.19
  307.1 7.8 multiply_convert_fusion.1
  316.6 6.7 fusion.12
  324.5 46.9 %reduce-scatter.11.cloned.1.call-done = f32[256,1152]{1,0:T(8,128)} async-done(((f32[1024,1152]{1,0:T(8,128)}), f32[256,1152]{1,0:T(8,128)}) %reduce-scatter.11.cloned.1.call-update) | async-done | bytes 1179664 | tf_op jit(solution)/shard_map/reduce_scatter | solution.py:451
  376.9 23.8 %all-gather.9.cloned.1.call-done = bf16[1024,1152]{1,0:T(8,128)(2,1)} async-done(((bf16[256,1152]{1,0:T(8,128)(2,1)}), bf16[1024,1152]{1,0:T(8,128)(2,1)}) %all-gather.9.cloned.1.call-update) | async-done | bytes 2359312 | tf_op jit(solution)/shard_map/all_gather | solution.py:458
  400.6 14.8 %multiply_convert_fusion = (bf16[1024,1728]{0,1:T(8,128)(2,1)S(1)}, bf16[1024,1728]{0,1:T(8,128)(2,1)S(1)}) fusion(f32[1024,1728]{0,1:T(8,128)} %copy-done.54, f32[1024,1728]{0,1:T(8,128)} %get-tuple-element.94, bf16[1024,1152]{1,0:T(8,128)(2,1)} %all-gather.9.cloned.1.call-done, bf16[1152,1792]{0,1:T(8,128)(2,1)} %bitcast.227), kind=kOutput, calls=%fused_computation.13 | convolution fusion | flops 4119330816 | bytes 27574272 | tf_op jit(solution)/shard_map/dot_general | solution.py:295
  420.9 6.8 convolution_add_fusion.2
  427.9 47.9 %reduce-scatter.13.cloned.1.call-done = f32[256,1152]{1,0:T(8,128)} async-done(((f32[1024,1152]{1,0:T(8,128)}), f32[256,1152]{1,0:T(8,128)}) %reduce-scatter.13.cloned.1.call-update) | async-done | bytes 1179664 | tf_op jit(solution)/shard_map/reduce_scatter | solution.py:465
  487.3 10.1 %convolution_convert_fusion = bf16[1152,1728]{0,1:T(8,128)(2,1)} fusion(bf16[1024,1728]{0,1:T(8,128)(2,1)} %copy-done.53, bf16[1024,1152]{1,0:T(8,128)(2,1)} %all-gather.9.cloned.1.call-done), kind=kOutput, calls=%fused_computation.3 | convolution fusion | flops 4078854144 | bytes 9879552 | tf_op jit(solution)/shard_map/dot_general | solution.py:289
  526.9 9.3 %convolution_convert_fusion.2 = bf16[1152,1728]{0,1:T(8,128)(2,1)} fusion(bf16[1024,1728]{0,1:T(8,128)(2,1)} %copy-done.52, bf16[1024,1152]{1,0:T(8,128)(2,1)S(1)} %copy-done.49), kind=kOutput, calls=%fused_computation.5 | convolution fusion | flops 4078854144 | bytes 9879552 | tf_op jit(solution)/shard_map/dot_general | solution.py:289
  538.5 6.5 copy.92
  549.3 6.5 copy.91
  560.1 6.5 copy.90
  566.6 10.5 %pad_maximum_fusion = bf16[7,1152,768]{2,1,0:T(8,128)(2,1)} fusion(bf16[7,1152,256]{2,1,0:T(8,128)(2,1)} %bitcast.210, bf16[7,1152,256]{2,1,0:T(8,128)(2,1)} %bitcast.211, bf16[7,1152,256]{2,1,0:T(8,128)(2,1)} %bitcast.212), kind=kLoop, calls=%fused_computation | loop fusion | flops 37158912 | bytes 24772608 | tf_op jit(solution)/shard_map/concatenate | solution.py:257
  587.6 155.4 %shard_map.272 = (f32[144,1024]{1,0:T(8,128)}, f32[7,144,768]{2,1,0:T(8,128)}) custom-call(bf16[8,144,1024]{2,1,0:T(8,128)(2,1)} %pad_maximum_fusion.1.attn_ref, bf16[7,8,144,768]{3,2,1,0:T(8,128)(2,1)} %bitcast.206), custom_call_target="tpu_custom_call" | custom-call | tf_op jit(solution)/shard_map/pallas_call | solution.py:219
  744.9 8.4 %fusion.93 = (f32[40,256]{1,0:T(8,128)S(1)}, f32[40,256]{1,0:T(8,128)S(1)}) fusion(f32[144,256]{1,0:T(8,128)S(1)} %get-tuple-element.76, f32[144,256]{1,0:T(8,128)S(1)} %get-tuple-element.75), kind=kCustom, calls=%all-reduce-scatter.2 | all-reduce-scatter fusion | flops 81921 | bytes 377344
  766.3 39.7 %all-reduce.21 = (f32[1152]{0:T(1024)S(1)}, f32[1152]{0:T(1024)S(1)}, f32[256]{0:T(256)S(1)}, f32[256]{0:T(256)S(1)}, f32[1152]{0:T(1024)S(1)}, /*index=5*/f32[1152]{0:T(1024)S(1)}) all-reduce(f32[1152]{0:T(1024)S(1)} %get-tuple-element.33, ...), channel_id=8, replica_groups=mesh['dp'=8,'tensor'=4] {'dp','tensor'}, use_global_device_ids=true, to_apply=%region_24.25.clone | all-reduce | flops 5120 | bytes 40960
  (261 shorter events, 134.2 us)
Async XLA Ops:
  7.2 6.1 copy-start.38
  7.2 6.1 copy-start.39
  7.2 6.1 copy-start.40
  7.2 194.9 %all-gather.5.cloned.1.call-start = ((), (), s32[]{:S(2)}) async-start(), calls=%async_computation.4 | async-start | bytes 2949120 | tf_op jit(solution)/shard_map/all_gather | solution.py:428
  14.8 163.0 %copy-start.5 = (bf16[256,1152]{1,0:T(8,128)(2,1)S(1)}, bf16[256,1152]{1,0:T(8,128)(2,1)}, u32[]{:S(2)}) copy-start(bf16[256,1152]{1,0:T(8,128)(2,1)} %param.16) | copy-start | bytes 1769476
  179.0 88.1 %reduce-scatter.9.cloned.1.call-start = ((), (), s32[]{:S(2)}) async-start(), calls=%async_computation.5 | async-start | bytes 5898240 | tf_op jit(solution)/shard_map/reduce_scatter | solution.py:439
  219.0 80.6 %all-gather.7.cloned.1.call-start = ((), (), s32[]{:S(2)}) async-start(), calls=%async_computation.6 | async-start | bytes 2949120 | tf_op jit(solution)/shard_map/all_gather | solution.py:445
  271.5 99.9 %reduce-scatter.11.cloned.1.call-start = ((), (), s32[]{:S(2)}) async-start(), calls=%async_computation.7 | async-start | bytes 5898240 | tf_op jit(solution)/shard_map/reduce_scatter | solution.py:451
  299.6 7.4 copy-start.13
  299.6 7.4 copy-start.47
  307.1 7.8 copy-start.54
  307.1 9.5 %copy-start.16 = (bf16[7,1152,256]{1,2,0:T(8,128)(2,1)S(1)}, bf16[7,1152,256]{1,2,0:T(8,128)(2,1)}, u32[]{:S(2)}) copy-start(bf16[7,1152,256]{1,2,0:T(8,128)(2,1)} %copy.105) | copy-start | bytes 12386308
  323.3 77.3 %all-gather.9.cloned.1.call-start = ((), (), s32[]{:S(2)}) async-start(), calls=%async_computation.8 | async-start | bytes 2949120 | tf_op jit(solution)/shard_map/all_gather | solution.py:458
  376.4 99.4 %reduce-scatter.13.cloned.1.call-start = ((), (), s32[]{:S(2)}) async-start(), calls=%async_computation.9 | async-start | bytes 5898240 | tf_op jit(solution)/shard_map/reduce_scatter | solution.py:465
  400.6 14.9 %copy-start.15 = (bf16[7,1152,256]{1,2,0:T(8,128)(2,1)S(1)}, bf16[7,1152,256]{1,2,0:T(8,128)(2,1)}, u32[]{:S(2)}) copy-start(bf16[7,1152,256]{1,2,0:T(8,128)(2,1)} %copy.103) | copy-start | bytes 12386308
  427.7 78.2 %all-gather.11.cloned.1.call-start = ((), (), s32[]{:S(2)}) async-start(), calls=%async_computation.10 | async-start | bytes 2949120 | tf_op jit(solution)/shard_map/all_gather | solution.py:475
  481.7 283.0 %reduce-scatter.15.cloned.1.call-start = ((), (), s32[]{:S(2)}) async-start(), calls=%async_computation.11 | async-start | bytes 2949120 | tf_op jit(solution)/shard_map/reduce_scatter | solution.py:496
  487.3 10.1 %copy-start.48 = (bf16[1024,1152]{1,0:T(8,128)(2,1)S(1)}, bf16[1024,1152]{1,0:T(8,128)(2,1)}, u32[]{:S(2)}) copy-start(bf16[1024,1152]{1,0:T(8,128)(2,1)} %all-gather.7.cloned.1.call-done) | copy-start | bytes 7077892
  487.3 10.1 %copy-start.56 = (bf16[1024,1728]{0,1:T(8,128)(2,1)S(1)}, bf16[1024,1728]{0,1:T(8,128)(2,1)}, u32[]{:S(2)}) copy-start(bf16[1024,1728]{0,1:T(8,128)(2,1)} %copy-done.55) | copy-start | bytes 10616836
  526.9 9.3 %copy-start.17 = (bf16[1152,1728]{0,1:T(8,128)(2,1)S(1)}, bf16[1152,1728]{0,1:T(8,128)(2,1)}, u32[]{:S(2)}) copy-start(bf16[1152,1728]{0,1:T(8,128)(2,1)} %convolution_convert_fusion) | copy-start | bytes 11943940
  566.6 10.5 %copy-start.21 = (bf16[1024,1152]{1,0:T(8,128)(2,1)S(1)}, bf16[1024,1152]{1,0:T(8,128)(2,1)}, u32[]{:S(2)}) copy-start(bf16[1024,1152]{1,0:T(8,128)(2,1)} %all-gather.11.cloned.1.call-done) | copy-start | bytes 7077892
  753.3 9.8 %collective-permute-start = (f32[12,256]{1,0:T(8,128)S(1)}, f32[12,256]{1,0:T(8,128)S(1)}, u32[]{:S(2)}, u32[]{:S(2)}) collective-permute-start(f32[12,256]{1,0:T(8,128)S(1)} %slice.147), channel_id=1, source_target_pairs={{0,1},{1,2},{2,3},{4,5},{5,6},{6,7},{8,9},{9,10},{10,11},{12,13},{... | collective-permute-start | bytes 36872
  754.7 8.6 %collective-permute-start.1 = (f32[12,256]{1,0:T(8,128)S(1)}, f32[12,256]{1,0:T(8,128)S(1)}, u32[]{:S(2)}, u32[]{:S(2)}) collective-permute-start(f32[12,256]{1,0:T(8,128)S(1)} %slice.148), channel_id=1, source_target_pairs={{0,1},{1,2},{2,3},{4,5},{5,6},{6,7},{8,9},{9,10},{10,11},{12,13},{... | collective-permute-start | bytes 36872
  762.1 47.4 %copy-start.9 = (f32[256,1152]{1,0:T(8,128)S(1)}, f32[256,1152]{1,0:T(8,128)}, u32[]{:S(2)}) copy-start(f32[256,1152]{1,0:T(8,128)} %copy-done.8) | copy-start | bytes 3538948
  (43 other events, 112.0 us)
Sparse Core Ops, SparseCore 0:
  179.1 22.9 all-gather.4
  219.2 47.9 reduce-scatter.8
  271.6 24.0 all-gather.6
  323.4 47.9 reduce-scatter.10
  376.6 24.0 all-gather.8
  427.8 47.9 reduce-scatter.12
  481.8 24.0 all-gather.10
  525.4 32.7 reduce-scatter.14

commit v2 on v1

--- a/solution.py
+++ b/solution.py
@@ -1,4 +1,3 @@
-import functools
 from functools import partial
 
 import jax
@@ -546,9 +545,761 @@
     )
 
 
+SCALE = HD**-0.5
+ROOT = 0.7978845608028654
+CUBIC = 0.044715
+
+
+def dot_nn(a, b):
+    return jnp.dot(a, b, preferred_element_type=F32)
+
+
+def dot_nt(a, b):
+    return lax.dot_general(a, b, (((1,), (1,)), ((), ())), preferred_element_type=F32)
+
+
+def dot_tn(a, b):
+    return lax.dot_general(a, b, (((0,), (0,)), ((), ())), preferred_element_type=F32)
+
+
+def inverse_rms(values):
+    return lax.rsqrt(jnp.mean(values * values, axis=-1, keepdims=True) + EPSILON)
+
+
+def rms_back(values, gain_vec, grad):
+    inverse = inverse_rms(values)
+    unit = values * inverse
+    scaled = grad * gain_vec
+    back = inverse * (scaled - unit * jnp.mean(scaled * unit, axis=-1, keepdims=True))
+    return back, grad * unit
+
+
+def gelu_parts(gate):
+    bent = jnp.tanh(ROOT * (gate + CUBIC * gate * gate * gate))
+    return 0.5 * gate * (1.0 + bent), bent
+
+
+class Quad:
+    def __init__(self, part, near, far, gather_sems, reduce_sems):
+        self.me = lax.axis_index("tensor")
+        self.twin = self.me + 1 - 2 * (self.me % 2)
+        self.across = (self.me + 2) % 4
+        self.corner = (self.twin + 2) % 4
+        self.part, self.near, self.far = part, near, far
+        self.gather_sems, self.reduce_sems = gather_sems, reduce_sems
+
+    def copy(self, src, dst, sems, use, k, peer):
+        return pltpu.make_async_remote_copy(
+            src,
+            dst,
+            sems[0].at[use, k],
+            sems[1].at[use, k],
+            device_id={"tensor": peer},
+            device_id_type=MESH,
+        )
+
+    def gather(self, use, k, buf):
+        block = buf.at[self.across if k == 2 else self.me]
+        peer = self.across if k == 1 else self.twin
+        return self.copy(block, block, self.gather_sems, use, k, peer)
+
+    def gather_start(self, use, buf):
+        self.gather(use, 1, buf).start()
+        self.gather(use, 0, buf).start()
+
+    def gather_relay(self, use, buf):
+        self.gather(use, 1, buf).wait_recv()
+        self.gather(use, 2, buf).start()
+
+    def gather_end(self, use, buf):
+        self.gather(use, 0, buf).wait_recv()
+        self.gather(use, 2, buf).wait_recv()
+        for k in range(3):
+            self.gather(use, k, buf).wait_send()
+
+    def reduce(self, use, k):
+        block = self.part.at[(self.twin, self.corner, self.across)[k]]
+        land = self.far if k == 2 else self.near.at[k]
+        peer = self.across if k == 2 else self.twin
+        return self.copy(block, land, self.reduce_sems, use, k, peer)
+
+    def reduce_start(self, use):
+        self.reduce(use, 1).start()
+        self.reduce(use, 0).start()
+
+    def reduce_relay(self, use):
+        self.reduce(use, 1).wait_recv()
+        for low in range(0, self.part.shape[1], 64):
+            rows = pl.ds(low, 64)
+            total = self.part[self.across, rows].astype(F32) + self.near[1, rows].astype(F32)
+            self.part[self.across, rows] = total.astype(BF)
+        self.reduce(use, 2).start()
+
+    def reduce_end(self, use):
+        self.reduce(use, 0).wait_recv()
+        self.reduce(use, 2).wait_recv()
+        for k in range(3):
+            self.reduce(use, k).wait_send()
+
+
+class Queue:
+    def __init__(self):
+        self.steps = []
+
+    def add(self, tag, fn):
+        self.steps.append((tag, fn))
+
+    def run(self, count, ready=None):
+        while count > 0 and self.steps:
+            tag, fn = self.steps[0]
+            if ready is not None and tag not in ready:
+                return
+            self.steps.pop(0)
+            fn()
+            count -= 1
+
+    def until(self, tag):
+        while any(t == tag for t, _ in self.steps):
+            self.run(1)
+
+
+def layer_kernel(
+    n,
+    x_ref,
+    cot_ref,
+    seg_row,
+    freq_ref,
+    gq_ref,
+    gk_ref,
+    attn_in,
+    ffn_in,
+    out_ref,
+    dx_ref,
+    sums_ref,
+    ggate_hbm,
+    gup_hbm,
+    gdown_hbm,
+    attn,
+    ffn,
+    attn_land,
+    ffn_land,
+    gate_buf,
+    up_buf,
+    hid_buf,
+    acc,
+    part,
+    near,
+    far,
+    xa,
+    nm,
+    df,
+    proj_s,
+    res_s,
+    gains,
+    gsum,
+    gqk,
+    q_proj,
+    k_proj,
+    qr,
+    kr,
+    vb,
+    att,
+    probs,
+    cos_s,
+    sin_s,
+    stage,
+    kvg,
+    kvg_land,
+    local_sem,
+    stage_sem,
+    ag_send,
+    ag_recv,
+    rs_send,
+    rs_recv,
+    qg_send,
+    qg_recv,
+    qr_send,
+    qr_recv,
+    kv_send,
+    kv_recv,
+):
+    chunks = ffn.shape[0]
+    rows, width = x_ref.shape
+    attn_cut = ((0, 2 * HD), (2 * HD, 4 * HD), (4 * HD, attn.shape[-1]))
+    ffn_cut = halves(ffn.shape[-1])
+    parts = part_views(attn, ffn, attn_cut, ffn_cut)
+    landing = part_views(attn_land, ffn_land, attn_cut, ffn_cut)
+    first = len(attn_cut)
+    ring = Ring(n, parts, ag_send, ag_recv)
+    back = Ring(n, parts, rs_send, rs_recv, lambda p, slot: landing[p](slot))
+    quad = Quad(part, near, far, (qg_send, qg_recv), (qr_send, qr_recv))
+    me = quad.me
+
+    def of_chunk(c):
+        return range(first + 2 * c, first + 2 * c + 2)
+
+    def piece(c, k):
+        return ffn[c, :, :, k * HD : (k + 1) * HD].reshape(width, HD)
+
+    def attn_cols(low, high):
+        return attn[:, :, low:high].reshape(width, high - low)
+
+    mine = [
+        pltpu.make_async_copy(attn_in, attn.at[ring.me], local_sem.at[0]),
+        pltpu.make_async_copy(ffn_in, ffn.at[:, ring.me], local_sem.at[1]),
+        pltpu.make_async_copy(x_ref, xa.at[me], local_sem.at[2]),
+    ]
+    for copy in mine:
+        copy.start()
+    barrier(ring.peer + [{"tensor": quad.twin}, {"tensor": quad.across}])
+    for copy in mine:
+        copy.wait()
+    quad.gather_start(0, xa)
+
+    queue = Queue()
+    slots = [[] for _ in range(2 * chunks + n + 4)]
+    for p in range(first):
+        for hop in range(1, n // 2 + 2):
+            slots[hop - 1].append((-1, p, hop))
+    for c in range(chunks):
+        for hop in range(1, n // 2 + 2):
+            for p in of_chunk(c):
+                slots[2 * (c + 1) + hop - 1].append((c, p, hop))
+    for slot in slots:
+        for c, p, hop in slot:
+            for way in range(2):
+                if hop <= ring.reach(p, way) + 1:
+                    queue.add(c, partial(ring.gather_step, p, way, hop))
+
+    queue.run(2 * first)
+    quarter = SEGMAX // 2
+
+    def seg_column(seg_j, half):
+        cut = seg_j[:, half * quarter : (half + 1) * quarter].astype(F32)
+        return jnp.transpose(jnp.broadcast_to(cut, (128, quarter)))[:, :1]
+
+    def tables(tile, _):
+        seg_j = seg_row[pl.ds(tile, 1), :]
+        for half in range(2):
+            r = 2 * tile + half
+            same = seg_column(seg_j, half) == seg_j.astype(F32)
+            j = lax.broadcasted_iota(jnp.int32, (quarter, SEGMAX), 1)
+            start = jnp.min(jnp.where(same, j, SEGMAX).astype(F32), axis=1, keepdims=True)
+            i = lax.broadcasted_iota(jnp.int32, (quarter, 1), 0).astype(F32) + half * quarter
+            angle = (i - start) * freq_ref[...]
+            cos_s[r] = jnp.cos(angle)
+            sin_s[r] = jnp.sin(angle)
+        return 0
+
+    lax.fori_loop(0, N_TILES, tables, 0)
+    quad.gather_relay(0, xa)
+    queue.until(-1)
+    flipped = jnp.transpose(attn_cols(4 * HD, 4 * HD + 128).astype(F32))
+    gains[...] = flipped[:8]
+    quad.gather_end(0, xa)
+    gain_in, gain_attn = gains[0:1, :], gains[1:2, :]
+    gain_pre, gain_post = gains[2:3, :], gains[3:4, :]
+    gain_q, gain_k = gq_ref[...], gk_ref[...]
+    queue.run(4)
+
+    sub = 32
+    per = rows // sub
+
+    def normalize(i, _):
+        b, at = i // per, pl.ds(pl.multiple_of(i % per * sub, sub), sub)
+        values = xa[b, at].astype(F32)
+        xa[b, at] = (values * inverse_rms(values) * gains[0:1, :]).astype(BF)
+        return 0
+
+    lax.fori_loop(0, 4 * per, normalize, 0)
+
+    def rope(values, gain_vec, r):
+        normed = values * inverse_rms(values) * gain_vec
+        low, high = normed[:, : HD // 2], normed[:, HD // 2 :]
+        cosine, sine = cos_s[r], sin_s[r]
+        return jnp.concatenate([low * cosine - high * sine, high * cosine + low * sine], axis=1)
+
+    queue.run(2)
+
+    def project(r, _):
+        block = xa[r]
+        query = dot_nn(block, attn_cols(HD, 2 * HD))
+        q_proj[r] = query.astype(BF)
+        qr[r] = rope(query, gq_ref[...], r).astype(BF)
+        key = dot_nn(block, attn_cols(2 * HD, 3 * HD))
+        k_proj[r] = key.astype(BF)
+        kr[r] = rope(key, gk_ref[...], r).astype(BF)
+        vb[r] = dot_nn(block, attn_cols(3 * HD, 4 * HD)).astype(BF)
+        return 0
+
+    lax.fori_loop(0, 4, project, 0)
+    queue.run(4)
+
+    def attend_tile(tile, _):
+        two = pl.ds(2 * tile, 2)
+        keys = kr[two].reshape(SEGMAX, HD)
+        values = vb[two].reshape(SEGMAX, HD)
+        seg_j = seg_row[pl.ds(tile, 1), :]
+        for half in range(2):
+            r = 2 * tile + half
+            scores = dot_nt(qr[r], keys) * SCALE
+            j = lax.broadcasted_iota(jnp.int32, (quarter, SEGMAX), 1)
+            i = lax.broadcasted_iota(jnp.int32, (quarter, SEGMAX), 0) + half * quarter
+            seen = (seg_column(seg_j, half) == seg_j.astype(F32)) & (i >= j)
+            scores = jnp.where(seen, scores, NEG_LARGE)
+            powers = jnp.exp(scores - jnp.max(scores, axis=1, keepdims=True))
+            weights = (powers / jnp.sum(powers, axis=1, keepdims=True)).astype(BF)
+            probs[r] = weights
+            att[r] = dot_nn(weights, values).astype(BF)
+        return 0
+
+    lax.fori_loop(0, N_TILES, attend_tile, 0)
+    queue.run(2)
+
+    def out_block(r, _):
+        acc[r] = dot_nt(att[r], attn_cols(0, HD))
+        part[r] = acc[r].astype(BF)
+        return 0
+
+    lax.fori_loop(0, 4, out_block, 0)
+    quad.reduce_start(0)
+    queue.run(2)
+    quad.reduce_relay(0)
+    queue.run(10)
+    quad.reduce_end(0)
+
+    def total(at):
+        return acc[me, at] + near[0, at].astype(F32) + far[at].astype(F32)
+
+    def at_rows(i):
+        return pl.ds(pl.multiple_of(i * sub, sub), sub)
+
+    def middle(i, _):
+        at = at_rows(i)
+        projected = total(at)
+        proj_s[at] = projected.astype(BF)
+        mid = x_ref[at].astype(F32) + projected * inverse_rms(projected) * gains[1:2, :]
+        res_s[at] = mid
+        nm[me, at] = (mid * inverse_rms(mid) * gains[2:3, :]).astype(BF)
+        return 0
+
+    lax.fori_loop(0, per, middle, 0)
+    quad.gather_start(1, nm)
+    queue.run(6)
+    quad.gather_relay(1, nm)
+    queue.run(4)
+    quad.gather_end(1, nm)
+
+    for c in range(chunks):
+        queue.until(c)
+
+        def ffn_block(r, _):
+            block = nm[r]
+            gate = dot_nn(block, piece(c, 0))
+            up = dot_nn(block, piece(c, 1))
+            gate_buf[c, r] = gate.astype(BF)
+            up_buf[c, r] = up.astype(BF)
+            hidden = (gelu_parts(gate)[0] * up).astype(BF)
+            grown = dot_nt(hidden, piece(c, 2))
+            if c > 0:
+                grown = grown + acc[r]
+            acc[r] = grown
+            if c == chunks - 1:
+                part[r] = grown.astype(BF)
+            return 0
+
+        lax.fori_loop(0, 4, ffn_block, 0)
+    queue.run(10**6)
+    quad.reduce_start(1)
+    for p in range(len(parts)):
+        ring.gather_sends_done(p)
+    quad.reduce_relay(1)
+    quad.reduce_end(1)
+    eight = (8, width)
+
+    def fold(values):
+        return jnp.sum(values.reshape(sub // 8, 8, values.shape[-1]), axis=0)
+
+    def after_feed(i, carry):
+        at = at_rows(i)
+        feed = total(at)
+        out_ref[at] = (res_s[at] + feed * inverse_rms(feed) * gains[3:4, :]).astype(BF)
+        grad, gain_part = rms_back(feed, gains[3:4, :], cot_ref[at].astype(F32))
+        df[me, at] = grad.astype(BF)
+        return carry + fold(gain_part)
+
+    gain_sum = lax.fori_loop(0, per, after_feed, jnp.zeros(eight, F32))
+    gsum[3:4, :] = jnp.sum(gain_sum, axis=0, keepdims=True)
+    quad.gather_start(2, df)
+    quad.gather_relay(2, df)
+    quad.gather_end(2, df)
+
+    queue = Queue()
+    slots = [[] for _ in range(2 * (chunks + 3) + n)]
+    for c in range(chunks):
+        for hop in range(1, n // 2 + 1):
+            for p in of_chunk(c):
+                slots[2 * c + hop].append((c, p, hop))
+    stage_count = [0]
+
+    def finish(c, p):
+        low = ffn_cut[(p - first) % 2]
+        k = stage_count[0]
+        stage_count[0] += 1
+        copies = []
+        for which, hbm in ((0, ggate_hbm), (1, gup_hbm), (2, gdown_hbm)):
+            left = max(low[0], which * HD)
+            right = min(low[1], (which + 1) * HD)
+            if left < right:
+                copies.append(
+                    pltpu.make_async_copy(
+                        stage.at[k % 2, :, pl.ds(left - low[0], right - left)],
+                        hbm.at[:, pl.ds(c * HD + left - which * HD, right - left)],
+                        stage_sem.at[k % 2, len(copies)],
+                    )
+                )
+        if k >= 2:
+            for copy in pending[k - 2]:
+                copy.wait()
+        stage[k % 2] = back.reduce_end(p)
+        for copy in copies:
+            copy.start()
+        pending.append(copies)
+
+    pending = []
+    for s, slot in enumerate(slots):
+        for c, p, hop in slot:
+            for way in range(2):
+                if hop <= back.reach(p, way):
+                    queue.add(c, partial(back.reduce_step, p, way, hop))
+        c = (s - n // 2 - 1) // 2
+        if s >= n // 2 + 1 and (s - n // 2 - 1) % 2 == 0 and c < chunks:
+            for p in of_chunk(c):
+                queue.add(c, partial(finish, c, p))
+    ready = set()
+
+    for c in range(chunks):
+
+        def back_block(r, _):
+            grad = dot_nn(df[r], piece(c, 2))
+            gate, up = gate_buf[c, r].astype(F32), up_buf[c, r].astype(F32)
+            act, bent = gelu_parts(gate)
+            slope = 0.5 * (1.0 + bent) + 0.5 * gate * (1.0 - bent * bent) * ROOT * (
+                1.0 + 3.0 * CUBIC * gate * gate
+            )
+            d_gate = (grad * up * slope).astype(BF)
+            d_up = (grad * act).astype(BF)
+            hid_buf[r] = (act * up).astype(BF)
+            gate_buf[c, r] = d_gate
+            up_buf[c, r] = d_up
+            grown = dot_nt(d_gate, piece(c, 0)) + dot_nt(d_up, piece(c, 1))
+            if c > 0:
+                grown = grown + acc[r]
+            acc[r] = grown
+            if c == chunks - 1:
+                part[r] = grown.astype(BF)
+            return 0
+
+        lax.fori_loop(0, 4, back_block, 0)
+        queue.run(PACE[0], ready)
+
+        def grad_piece(k, left, right):
+            value = dot_tn(left.reshape(4 * rows, width), right.reshape(4 * rows, HD))
+            ffn[c, :, :, k * HD : (k + 1) * HD] = value.astype(BF).reshape(n, width // n, HD)
+
+        grad_piece(2, df[...], hid_buf[...])
+        if c == chunks - 1:
+            quad.reduce_start(2)
+        queue.run(PACE[1], ready)
+        grad_piece(0, nm[...], gate_buf[c])
+        queue.run(PACE[1], ready)
+        if c == chunks - 1:
+            quad.reduce_relay(2)
+        grad_piece(1, nm[...], up_buf[c])
+        ready.add(c)
+        queue.run(PACE[1], ready)
+
+    queue.run(PACE[2], ready)
+    quad.reduce_end(2)
+
+    def after_ffn(i, carry):
+        at = at_rows(i)
+        grad, pre_part = rms_back(res_s[at], gains[2:3, :], total(at))
+        grad = cot_ref[at].astype(F32) + grad
+        res_s[at] = grad
+        grad, attn_part = rms_back(proj_s[at].astype(F32), gains[1:2, :], grad)
+        df[me, at] = grad.astype(BF)
+        return carry[0] + fold(pre_part), carry[1] + fold(attn_part)
+
+    zero = jnp.zeros(eight, F32)
+    pre_sum, attn_sum = lax.fori_loop(0, per, after_ffn, (zero, zero))
+    gsum[2:3, :] = jnp.sum(pre_sum, axis=0, keepdims=True)
+    gsum[1:2, :] = jnp.sum(attn_sum, axis=0, keepdims=True)
+    quad.gather_start(3, df)
+    queue.run(PACE[3], ready)
+    quad.gather_relay(3, df)
+    queue.run(PACE[4], ready)
+    quad.gather_end(3, df)
+
+    d_q, d_k, d_v, datt = (gate_buf.at[k] for k in range(4))
+    def back_out(r, _):
+        datt[r] = dot_nn(df[r], attn_cols(0, HD)).astype(BF)
+        return 0
+
+    lax.fori_loop(0, 4, back_out, 0)
+    queue.run(PACE[5], ready)
+    gqk[...] = jnp.zeros_like(gqk)
+
+    def unrope(grad, projection, gain_vec, r, row):
+        low, high = grad[:, : HD // 2], grad[:, HD // 2 :]
+        cosine, sine = cos_s[r], sin_s[r]
+        grad = jnp.concatenate([low * cosine + high * sine, high * cosine - low * sine], axis=1)
+        grad, gain_part = rms_back(projection, gain_vec, grad)
+        gqk[row : row + 1, :] += jnp.sum(gain_part, axis=0, keepdims=True)
+        return grad.astype(BF)
+
+    def back_tile(tile, _):
+        two = pl.ds(2 * tile, 2)
+        keys = kr[two].reshape(SEGMAX, HD)
+        values = vb[two].reshape(SEGMAX, HD)
+        d_key = jnp.zeros((SEGMAX, HD), F32)
+        d_value = jnp.zeros((SEGMAX, HD), F32)
+        for half in range(2):
+            r = 2 * tile + half
+            d_att = datt[r]
+            weights = probs[r]
+            d_value = d_value + dot_tn(weights, d_att)
+            d_probs = dot_nt(d_att, values)
+            weights = weights.astype(F32)
+            delta = jnp.sum(weights * d_probs, axis=1, keepdims=True)
+            d_scores = (weights * (d_probs - delta) * SCALE).astype(BF)
+            d_key = d_key + dot_tn(d_scores, qr[r])
+            d_query = dot_nn(d_scores, keys)
+            d_q[r] = unrope(d_query, q_proj[r].astype(F32), gq_ref[...], r, 4)
+        for half in range(2):
+            r = 2 * tile + half
+            cut = slice(half * quarter, (half + 1) * quarter)
+            d_k[r] = unrope(d_key[cut], k_proj[r].astype(F32), gk_ref[...], r, 5)
+            d_v[r] = d_value[cut].astype(BF)
+        return 0
+
+    lax.fori_loop(0, N_TILES, back_tile, 0)
+    queue.run(PACE[5], ready)
+
+    def back_in(r, _):
+        grown = dot_nt(d_q[r], attn_cols(HD, 2 * HD))
+        grown = grown + dot_nt(d_k[r], attn_cols(2 * HD, 3 * HD))
+        grown = grown + dot_nt(d_v[r], attn_cols(3 * HD, 4 * HD))
+        acc[r] = grown
+        part[r] = grown.astype(BF)
+        return 0
+
+    lax.fori_loop(0, 4, back_in, 0)
+    quad.reduce_start(3)
+    queue.run(PACE[5], ready)
+
+    def attn_grad(low, left, right):
+        value = dot_tn(left.reshape(4 * rows, width), right.reshape(4 * rows, HD))
+        attn[:, :, low : low + HD] = value.astype(BF).reshape(n, width // n, HD)
+
+    attn_grad(0, df[...], att[...])
+    quad.reduce_relay(3)
+    for k, grad in enumerate((d_q, d_k, d_v)):
+        attn_grad((k + 1) * HD, xa[...], grad[...])
+        queue.run(PACE[5], ready)
+    queue.run(PACE[6], ready)
+    quad.reduce_end(3)
+
+    def after_attn(i, carry):
+        at = at_rows(i)
+        grad, gain_part = rms_back(x_ref[at].astype(F32), gains[0:1, :], total(at))
+        dx_ref[at] = (res_s[at] + grad).astype(BF)
+        return carry + fold(gain_part)
+
+    gain_sum = lax.fori_loop(0, per, after_attn, zero)
+    gsum[0:1, :] = jnp.sum(gain_sum, axis=0, keepdims=True)
+    gsum[4:8, :] = jnp.zeros((4, width), F32)
+    tall = jnp.concatenate([gsum[...], jnp.zeros((120, width), F32)], axis=0)
+    tall = jnp.transpose(tall).reshape(n, width // n, 128)
+    short = jnp.concatenate([gqk[...], jnp.zeros((120, HD), F32)], axis=0)
+    short = jnp.transpose(short).reshape(n, HD // n, 128)
+    attn[:, :, 4 * HD : 4 * HD + 128] = tall.astype(BF)
+    attn[:, : HD // n, 4 * HD : 4 * HD + 128] = (tall[:, : HD // n] + short).astype(BF)
+
+    for hop in range(1, n // 2 + 1):
+        for p in range(first):
+            for way in range(2):
+                if hop <= back.reach(p, way):
+                    queue.add(-1, partial(back.reduce_step, p, way, hop))
+    queue.run(10**6)
+    sums_ref[:, : 2 * HD] = back.reduce_end(0)
+    kvg[0, :, : 2 * HD] = back.reduce_end(1).astype(BF)
+    kvg[0, :, 2 * HD :] = back.reduce_end(2).astype(BF)
+    for k, peer in enumerate((quad.twin, quad.across)):
+        copy = pltpu.make_async_remote_copy(
+            kvg.at[k],
+            kvg_land.at[k],
+            kv_send.at[k],
+            kv_recv.at[k],
+            device_id={"tensor": peer},
+            device_id_type=MESH,
+        )
+        copy.start()
+        copy.wait()
+        grown = kvg[k].astype(F32) + kvg_land[k].astype(F32)
+        if k == 0:
+            kvg[1] = grown.astype(BF)
+        else:
+            sums_ref[:, 2 * HD :] = grown
+    for p in range(len(parts)):
+        back.reduce_sends_done(p)
+    for copies in pending[-2:]:
+        for copy in copies:
+            copy.wait()
+
+
+PACE = (1, 1, 2, 6, 4, 1, 4)
+N_TILES = 2
+
+
+def run_layer(n, x, cot, segments, g_query, g_key, attn_pack, ffn_pack):
+    rows, width = x.shape
+    chunks, depth, cols = ffn_pack.shape
+    tokens = segments.shape[0]
+    wide = attn_pack.shape[1]
+    parts = 3 + 2 * chunks
+    exponent = -2.0 * jnp.arange(HD // 2, dtype=F32) / HD
+    freq = jnp.power(jnp.float32(THETA), exponent)[None, :]
+    vmem, dma = pltpu.VMEM, pltpu.SemaphoreType.DMA
+    grown = chunks * HD
+    return pl.pallas_call(
+        partial(layer_kernel, n),
+        out_shape=(
+            jax.ShapeDtypeStruct((rows, width), BF),
+            jax.ShapeDtypeStruct((rows, width), BF),
+            jax.ShapeDtypeStruct((depth, wide), F32),
+            jax.ShapeDtypeStruct((depth, grown), F32),
+            jax.ShapeDtypeStruct((depth, grown), F32),
+            jax.ShapeDtypeStruct((depth, grown), F32),
+        ),
+        in_specs=vmem_specs(6) + any_specs(2),
+        out_specs=vmem_specs(3) + any_specs(3),
+        scratch_shapes=[
+            vmem((n, depth, wide), BF),
+            vmem((chunks, n, depth, cols), BF),
+            vmem((n - 1, depth, wide), BF),
+            vmem((chunks, n - 1, depth, cols), BF),
+            vmem((chunks, 4, rows, HD), BF),
+            vmem((chunks, 4, rows, HD), BF),
+            vmem((4, rows, HD), BF),
+            vmem((4, rows, width), F32),
+            vmem((4, rows, width), BF),
+            vmem((2, rows, width), BF),
+            vmem((rows, width), BF),
+            vmem((4, rows, width), BF),
+            vmem((4, rows, width), BF),
+            vmem((4, rows, width), BF),
+            vmem((rows, width), BF),
+            vmem((rows, width), F32),
+            vmem((8, width), F32),
+            vmem((8, width), F32),
+            vmem((8, HD), F32),
+            vmem((4, rows, HD), BF),
+            vmem((4, rows, HD), BF),
+            vmem((4, rows, HD), BF),
+            vmem((4, rows, HD), BF),
+            vmem((4, rows, HD), BF),
+            vmem((4, rows, HD), BF),
+            vmem((4, rows, SEGMAX), BF),
+            vmem((4, rows, HD // 2), F32),
+            vmem((4, rows, HD // 2), F32),
+            vmem((2, depth, cols // 2), F32),
+            vmem((2, depth, wide - 2 * HD), BF),
+            vmem((2, depth, wide - 2 * HD), BF),
+            dma((3,)),
+            dma((2, 2)),
+            dma((parts, 2, n // 2)),
+            dma((parts, 2, n // 2)),
+            dma((parts, 2, n // 2)),
+            dma((parts, 2, n // 2)),
+            dma((4, 3)),
+            dma((4, 3)),
+            dma((4, 3)),
+            dma((4, 3)),
+            dma((2,)),
+            dma((2,)),
+        ],
+        compiler_params=pltpu.CompilerParams(
+            collective_id=2, has_side_effects=True, vmem_limit_bytes=67043328
+        ),
+    )(
+        x,
+        cot,
+        segments.reshape(N_TILES, SEGMAX),
+        freq,
+        g_query.astype(F32)[None, :],
+        g_key.astype(F32)[None, :],
+        attn_pack,
+        ffn_pack,
+    )
+
+
+def fused_local(
+    inputs, segments, w_query, w_key, w_value, w_out, g_in, g_attn, g_query, g_key,
+    w_gate, w_up, w_down, g_pre, g_post, cotangent,
+):
+    n = lax.axis_size("dp")
+    depth = w_query.shape[0]
+    width = w_gate.shape[1]
+    gains = jnp.stack([g_in, g_attn, g_pre, g_post], axis=1)
+    attn_pack = jnp.concatenate(
+        [w_out.T, w_query, w_key, w_value, jnp.pad(gains, ((0, 0), (0, 124)))], axis=1
+    )
+    ffn_pack = pack_ffn(w_gate, w_up, w_down.T, depth)
+    output, d_inputs, sums, g_gate, g_up, g_down = run_layer(
+        n, inputs, cotangent, segments, g_query, g_key, attn_pack, ffn_pack
+    )
+    spot = lax.axis_index("tensor")
+    part = depth // 4
+    mine = lax.dynamic_slice_in_dim(sums[:, 2 * HD :], spot * part, part, 0)
+    small = HD // n // 4
+    few = lax.dynamic_slice_in_dim(sums[:, 4 * HD :], spot * small, small, 0)
+    return (
+        output,
+        d_inputs,
+        sums[:, HD : 2 * HD],
+        mine[:, :HD],
+        mine[:, HD : 2 * HD],
+        sums[:, :HD].T,
+        mine[:, 2 * HD],
+        mine[:, 2 * HD + 1],
+        few[:, 4],
+        few[:, 5],
+        g_gate[:, :width],
+        g_up[:, :width],
+        g_down[:, :width].T,
+        mine[:, 2 * HD + 2],
+        mine[:, 2 * HD + 3],
+    )
+
+
+def fits(mesh, depth, tokens, rows):
+    return depth % 16 == 0 and mesh.shape["tensor"] == 4 and tokens == 2 * SEGMAX
+
+
+def layer(mesh):
+    def body(*args):
+        inputs, segments, w_query = args[0], args[1], args[2]
+        if fits(mesh, w_query.shape[0], segments.shape[0], inputs.shape[0]):
+            return fused_local(*args)
+        return local(*args)
+
+    return body
+
+
 def solution(mesh):
     return jax.shard_map(
-        local,
+        layer(mesh),
         mesh=mesh,
         in_specs=(
             P(("dp", "tensor"), None),

time: 829 us -> 472 us (0.57)
  waiting for transfers between devices: 187 us -> 0 us
  Pallas kernels: 315 us -> 442 us
  matrix products: 102 us -> 0 us
  local copies, waits for them, and re-layouts: 102 us -> 16.9 us
  blocking collectives: 48.2 us -> 0 us
  other arithmetic: 42.4 us -> 2.93 us
  between operations: 16.2 us -> 1.32 us
    reduce_scatter x4 -> x0, waiting for transfers between devices: 142 us -> none  [the longest x1 47.9 us: local(): lax.psum_scatter(cols_product(d_gate, wg_back) + cols_product(d_up, wu_ba...]
    pallas_call x2 -> x1, Pallas kernels: 315 us -> 442 us  [run_layer(): pl.pallas_call(partial(layer_kernel, n), out_shape=(jax.ShapeDtypeStruct(...]
    dot_general x27 -> x0, matrix products: 102 us -> none  [the longest x7 33.8 us: cols_product(): lax.dot_general(left, right, (((1,), (1,)), ((), ())), preferred_element_...]
    unnamed x2 -> x0, blocking collectives: 48.2 us -> none
    all_gather x4 -> x0, waiting for transfers between devices: 45.3 us -> none  [the longest x1 23.8 us: local(): lax.all_gather(d_feed_f.astype(jnp.bfloat16), 'tensor', axis=0, tiled=True)]
    unnamed x139 -> x42, local copies, waits for them, and re-layouts: 41.7 us -> 6.2 us
    reshape x4 -> x1, local copies, waits for them, and re-layouts: 19.4 us -> 0.04 us  [cut(): return array.reshape(rows, chunks, CHUNK).transpose(1, 0, 2)]
    reduce_sum x10 -> x0, other arithmetic: 14 us -> none  [the longest x5 8.75 us: rms_scale(): return values * inverse * gain_vec]
  transfers between devices with their start and end apart: 10 -> 0, of which waited for: 6 -> 0; matrix products, arithmetic and copies ran while one was open for 16% -> 0% of each run, Pallas kernels for 19% -> 0%
where the time goes in v2:
time: 472 us; the launch traced here: 463 us
  Pallas kernels  442 us (94%)
  local copies, waits for them, and re-layouts  16.9 us (4%)
    pallas_call x1, Pallas kernels, run_layer(): pl.pallas_call(partial(layer_kernel, n), out_shape=(jax.ShapeDtypeStruct(...  442 us

profile of v2, /device:TPU:0, one launch (start us, length us, event | category | flops | bytes accessed | tf_op | source)
XLA Modules:
  0.0 463.1 jit_solution(2358782188259024986)
XLA Ops:
  0.6 1.1 pad.16
  1.7 1.1 pad.17
  3.2 1.3 pad_maximum_fusion.ffn_in
  4.5 0.6 bitcast_dynamic-update-slice_fusion
  5.1 0.6 constant_dynamic-update-slice_fusion.2
  5.7 0.6 constant_dynamic-update-slice_fusion.1
  6.4 0.6 constant_dynamic-update-slice_fusion
  7.2 0.6 pad_dynamic-update-slice_fusion.attn_in
  7.9 0.6 reshape.52.seg_row
  8.5 0.6 broadcast_in_dim.15
  9.1 0.6 broadcast_in_dim.16
  9.6 0.5 multiply_power_fusion.freq_ref
  10.1 442.0 %shard_map.271 = (bf16[256,1152]{1,0:T(8,128)(2,1)}, bf16[256,1152]{1,0:T(8,128)(2,1)}, f32[144,1152]{1,0:T(8,128)}, f32[144,1792]{1,0:T(8,128)}, f32[144,1792]{1,0:T(8,128)}, /*index=5*/f32[144,1792]{1,0:T(8,128)}) custom-call(bf16[256,1152]{1,0:T(8,128)(2,1)} %x_ref.1, bf16[256,1152]{1,0:T(8,128)(2,1)} %cot_ref.1, s32[2,512]{1,0:T(2,128)} %reshape.52.seg_row, ...), custom_call_target="tpu_custom_call" | custom-call | tf_op jit(solution)/shard_map/pallas_call | solution.py:1175
  452.2 1.1 slice.46
  453.3 0.8 dynamic-slice_reduce_fusion
  454.0 0.7 fusion
  454.7 0.9 slice.52
  455.6 0.7 slice_reduce_fusion
  456.4 1.7 slice_bitcast_fusion.1
  458.1 1.0 slice_bitcast_fusion
  459.1 0.8 copy.57
  459.9 0.8 copy.58
  460.7 1.0 copy.59
  461.7 1.0 copy.60
  (44 shorter events, 0.4 us)
Async XLA Ops:
  1.7 1.2 copy-start.5
  3.1 1.4 copy-start.6
  3.1 2.0 copy-start.7
  3.1 2.7 copy-start.8
  3.1 3.3 copy-start.9
  3.1 3.9 copy-start.11
  3.1 3.9 copy-start.12
  3.1 3.9 copy-start.13
  3.1 3.9 copy-start.14
  3.2 4.7 %copy-start.10 = (s32[1024]{0:T(1024)S(1)}, s32[1024]{0:T(1024)}, u32[]{:S(2)}) copy-start(s32[1024]{0:T(1024)} %param.17) | copy-start | bytes 12292
  3.2 5.3 %copy-start.15 = (bf16[256]{0:T(256)(128)(2,1)S(1)}, bf16[256]{0:T(256)(128)(2,1)}, u32[]{:S(2)}) copy-start(bf16[256]{0:T(256)(128)(2,1)} %param.24) | copy-start | bytes 1540
  3.2 5.9 %copy-start.16 = (bf16[256]{0:T(256)(128)(2,1)S(1)}, bf16[256]{0:T(256)(128)(2,1)}, u32[]{:S(2)}) copy-start(bf16[256]{0:T(256)(128)(2,1)} %param.25) | copy-start | bytes 1540
  452.1 5.9 %copy-start.2 = (f32[144,1792]{1,0:T(8,128)S(1)}, f32[144,1792]{1,0:T(8,128)}, u32[]{:S(2)}) copy-start(f32[144,1792]{1,0:T(8,128)} %get-tuple-element.26) | copy-start | bytes 3096580
  453.3 5.8 %copy-start.4 = (bf16[256,1152]{1,0:T(8,128)(2,1)S(1)}, bf16[256,1152]{1,0:T(8,128)(2,1)}, u32[]{:S(2)}) copy-start(bf16[256,1152]{1,0:T(8,128)(2,1)} %get-tuple-element.54) | copy-start | bytes 1769476
  458.1 1.9 copy-start.3
  459.1 1.6 copy-start.1
  459.9 1.8 copy-start
